TPU v7x, 32 devices: a whole 2x2x4 slice. The times are simulated.
32 devices in a mesh: ep: 32 (over z, y, x, core).
Axes of the slice: x: 2, y: 2, z: 4, core: 2. Of those that a mesh axis runs over, the one named last changes fastest.
Arguments:
- table_in: float32 [131072, 500], P('ep')
- table_out: float32 [131072, 500], P('ep')
- centers: int32 [32768], P('ep')
- contexts: int32 [32768], P('ep')
- negatives: int32 [32768, 15], P('ep')
Outputs:
- output 1: float32 [], replicated
- output 2: float32 [131072, 500], P('ep')
- output 3: float32 [131072, 500], P('ep')
All inputs are finite; a program needn't handle non-finite values.
Results may differ from a plain program's by a relative error of at most 0.001.
Values sent between devices are 32-bit elements.
A program may use at most 1 GiB of HBM per device.

v0:
```python
import jax
import jax.numpy as jnp
from jax import lax
from jax.sharding import PartitionSpec as P

LEARN_RATE = 0.5


def solution(mesh):
    group_size = mesh.shape['ep']

    def device_step(table_in, table_out, centers, contexts, negatives):
        rows_dev, width = table_in.shape
        n_pairs, n_neg = negatives.shape
        n_look = n_pairs * (n_neg + 2)
        capacity = (3 * n_look) // (2 * group_size)
        word_ids = jnp.concatenate([centers, contexts, negatives.reshape(n_pairs * n_neg)])
        owners = word_ids % group_size
        lookup_ids = jnp.arange(n_look)
        stack_row = word_ids // group_size + jnp.where(lookup_ids < n_pairs, 0, rows_dev)
        sort_order = jnp.argsort(owners, stable=True)
        owner_counts = jnp.bincount(owners, length=group_size)
        owner_starts = jnp.cumsum(owner_counts) - owner_counts
        owner_sorted = owners[sort_order]
        slot_sorted = owner_sorted * capacity + lookup_ids - owner_starts[owner_sorted]
        slot_of = jnp.zeros((n_look,), jnp.int32).at[sort_order].set(slot_sorted.astype(jnp.int32))
        rank_ids = jnp.arange(capacity)
        filled = rank_ids[None, :] < owner_counts[:, None]
        source = sort_order[jnp.minimum(owner_starts[:, None] + rank_ids[None, :], n_look - 1)]
        requests = jnp.where(filled, stack_row[source], 0).astype(jnp.int32)
        incoming = lax.all_to_all(requests, 'ep', 0, 0)
        stacked = jnp.concatenate([table_in, table_out], axis=0)
        served = stacked[incoming]
        fetched = lax.all_to_all(served, 'ep', 0, 0).reshape(group_size * capacity, width)
        looked = fetched[slot_of]
        u_vec = looked[:n_pairs]
        ctx_vec = looked[n_pairs:2 * n_pairs]
        neg_vec = looked[2 * n_pairs:].reshape(n_pairs, n_neg, width)
        pos_score = jnp.sum(u_vec * ctx_vec, axis=-1)
        neg_score = jnp.sum(u_vec[:, None, :] * neg_vec, axis=-1)
        local_loss = -jnp.sum(jax.nn.log_sigmoid(pos_score)) - jnp.sum(jax.nn.log_sigmoid(-neg_score))
        pos_coef = jax.nn.sigmoid(pos_score) - 1.0
        neg_coef = jax.nn.sigmoid(neg_score)
        grad_u = pos_coef[:, None] * ctx_vec + jnp.sum(neg_coef[:, :, None] * neg_vec, axis=1)
        grad_ctx = pos_coef[:, None] * u_vec
        grad_neg = (neg_coef[:, :, None] * u_vec[:, None, :]).reshape(n_pairs * n_neg, width)
        grad_rows = jnp.concatenate([grad_u, grad_ctx, grad_neg], axis=0)
        outgoing = jnp.where(filled[:, :, None], grad_rows[source], 0.0)
        returned = lax.all_to_all(outgoing, 'ep', 0, 0)
        grad_stack = jax.ops.segment_sum(returned.reshape(group_size * capacity, width),
                                         incoming.reshape(group_size * capacity), num_segments=2 * rows_dev)
        total_loss = lax.psum(local_loss, 'ep') / (n_pairs * group_size)
        new_in = table_in - LEARN_RATE * grad_stack[:rows_dev]
        new_out = table_out - LEARN_RATE * grad_stack[rows_dev:]
        return total_loss, new_in, new_out

    return jax.shard_map(device_step, mesh=mesh,
                         in_specs=(P('ep', None), P('ep', None), P('ep'), P('ep'), P('ep', None)),
                         out_specs=(P(), P('ep', None), P('ep', None)), check_vma=False)
```

profile of v0, /device:TPU:0, one launch (start us, length us, event | category | flops | bytes accessed | tf_op | source)
XLA Modules:
  0.0 3513.1 jit_solution(11504851919760312965)
XLA Ops:
  4.9 121.0 %scatter_custom_fusion = s32[32]{0:T(128)S(1)} fusion(s32[17408]{0:T(1024)S(1)} %bitcast.48, s32[17408]{0:T(1024)S(1)} %broadcast.314, s32[]{:T(128)} %constant.33.clone.1), kind=kCustom, calls=%fused_computation.98 | custom fusion | flops 17408 | bytes 132 | tf_op jit(solution)/shard_map/scatter-add | solution.py:22
  127.3 11.3 sort.17
  138.6 134.1 %gather_fusion = s32[26112]{0:T(1024)S(1)} fusion(s32[17408]{0:T(1024)S(1)} %get-tuple-element.4, s32[26624]{0:T(1024)S(1)} %pad_clamp_fusion.2), kind=kCustom, calls=%fused_computation | custom fusion | bytes 313344 | tf_op jit(solution)/shard_map/gather | solution.py:29
  273.5 133.9 %gather_fusion.1 = s32[26112]{0:T(1024)S(1)} fusion(s32[17408]{0:T(1024)S(1)} %get-tuple-element.46, s32[26624]{0:T(1024)S(1)} %pad_clamp_fusion.1), kind=kCustom, calls=%fused_computation.1 | custom fusion | bytes 313344 | tf_op jit(solution)/shard_map/gather | solution.py:30
  433.9 11.6 pad_maximum_fusion.1
  446.0 83.3 %gather_fusion.2 = f32[26112,500]{1,0:T(8,128)} fusion(f32[8192,500]{1,0:T(8,128)} %pad_maximum_fusion.1, s32[26624]{0:T(1024)S(1)} %pad_clamp_fusion), kind=kCustom, calls=%fused_computation.2 | custom fusion | bytes 104552448 | tf_op jit(solution)/shard_map/gather | solution.py:33
  536.1 96.2 %gather_fusion.3 = s32[17408]{0:T(1024)S(1)} fusion(s32[17408]{0:T(1024)S(1)} %copy-done.3, s32[17408]{0:T(1024)S(1)} %get-tuple-element.43), kind=kCustom, calls=%fused_computation.3 | custom fusion | bytes 208896 | tf_op jit(solution)/shard_map/gather | solution.py:24
  643.5 15.6 select_subtract_fusion
  659.2 64.1 %scatter_custom_fusion.1 = s32[17408]{0:T(1024)S(1)} fusion(s32[17408]{0:T(1024)S(1)} %get-tuple-element.44, s32[17408]{0:T(1024)S(1)} %select_subtract_fusion, s32[]{:T(128)} %constant.33.clone.1), kind=kCustom, calls=%fused_computation.90 | custom fusion | bytes 69636 | tf_op jit(solution)/shard_map/scatter | solution.py:26
  724.0 913.6 %all-to-all-done.1 = f32[32,816,500]{2,1,0:T(8,128)} async-done(((f32[32,816,500]{2,1,0:T(8,128)}), f32[32,816,500]{2,1,0:T(8,128)}, u32[]{:S(2)}, u32[]{:S(2)}) %all-to-all-start.1) | async-done | bytes 52224032 | tf_op jit(solution)/shard_map/all_to_all | solution.py:34
  1637.6 89.7 %gather_fusion.4 = f32[17408,500]{1,0:T(8,128)} fusion(f32[26112,500]{1,0:T(8,128)} %bitcast.6, s32[17408]{0:T(1024)S(1)} %fusion.8), kind=kCustom, calls=%fused_computation.4 | custom fusion | bytes 69701632 | tf_op jit(solution)/shard_map/gather | solution.py:35
  1729.7 11.4 mul.63
  1741.1 31.9 mul.64
  1773.0 31.3 fusion.19
  1805.0 23.4 broadcast_multiply_fusion
  1829.4 32.3 reshape.378
  1861.7 14.4 multiply_reduce_fusion
  1878.7 26.7 pad_maximum_fusion
  1905.5 88.6 %gather_fusion.5 = f32[26112,500]{1,0:T(8,128)} fusion(f32[17408,500]{1,0:T(8,128)} %pad_maximum_fusion, s32[26624]{0:T(1024)S(1)} %copy-done.5), kind=kCustom, calls=%fused_computation.5 | custom fusion | bytes 104552448 | tf_op jit(solution)/shard_map/gather | solution.py:48
  1994.1 35.8 %broadcast_select_fusion = f32[32,816,500]{2,1,0:T(8,128)} fusion(f32[32,816,500]{2,1,0:T(8,128)} %bitcast.45, pred[32,816]{1,0:T(8,128)(4,1)S(1)} %copy-done.10), kind=kLoop, calls=%fused_computation.12 | loop fusion | flops 13056000 | bytes 104474112 | tf_op jit(solution)/shard_map/jit(_where)/select_n | solution.py:48
  2029.8 77.2 %all-to-all-start.2 = ((f32[32,816,500]{2,1,0:T(8,128)}), f32[32,816,500]{2,1,0:T(8,128)}, u32[]{:S(2)}, u32[]{:S(2)}) async-start(f32[32,816,500]{2,1,0:T(8,128)} %broadcast_select_fusion), calls=%async_computation.2 | async-start | bytes 106954752 | tf_op jit(solution)/shard_map/all_to_all | solution.py:49
  2108.8 1195.8 %psum.7 = f32[]{:T(128)} all-reduce(f32[]{:T(128)S(6)} %sub.27), channel_id=1, replica_groups=mesh['ep'=32] {'ep'}, use_global_device_ids=true, to_apply=%region_8.9 | all-reduce | flops 1 | bytes 8 | tf_op jit(solution)/shard_map/psum | solution.py:52
  3305.2 169.9 %scatter_custom_fusion.2 = f32[8192,500]{1,0:T(8,128)} fusion(s32[26112]{0:T(1024)S(1)} %reshape.485, f32[26112,500]{1,0:T(8,128)} %bitcast.42, f32[]{:T(128)} %constant.69.clone.1), kind=kCustom, calls=%fused_computation.19 | custom fusion | flops 13056000 | bytes 16384512 | tf_op jit(solution)/shard_map/scatter-add | solution.py:50
  3475.1 18.9 fusion
  (74 shorter events, 76.9 us)
Async XLA Ops:
  3.9 268.9 %copy-start.2 = (s32[17408]{0:T(1024)}, s32[17408]{0:T(1024)S(1)}, u32[]{:S(2)}) copy-start(s32[17408]{0:T(1024)S(1)} %get-tuple-element.45) | copy-start | bytes 208900
  125.9 281.7 %copy-start.11 = (s32[32]{0:T(128)}, s32[32]{0:T(128)S(1)}, u32[]{:S(2)}) copy-start(s32[32]{0:T(128)S(1)} %scatter_custom_fusion) | copy-start | bytes 388
  126.2 0.5 copy-start.8
  138.6 134.1 %copy-start = (s32[17408]{0:T(1024)}, s32[17408]{0:T(1024)S(1)}, u32[]{:S(2)}) copy-start(s32[17408]{0:T(1024)S(1)} %get-tuple-element.4) | copy-start | bytes 208900
  273.5 134.0 %copy-start.4 = (s32[26624]{0:T(1024)}, s32[26624]{0:T(1024)S(1)}, u32[]{:S(2)}) copy-start(s32[26624]{0:T(1024)S(1)} %pad_clamp_fusion.1) | copy-start | bytes 319492
  408.4 37.0 %all-to-all-start = ((s32[32,1,816]{2,1,0:T(1,128)}), s32[32,1,816]{2,1,0:T(1,128)S(1)}, u32[]{:S(2)}, u32[]{:S(2)}) async-start(s32[32,1,816]{2,1,0:T(1,128)} %compare_select_fusion.3), calls=%async_computation | async-start | bytes 229376 | tf_op jit(solution)/shard_map/all_to_all | solution.py:31
  445.5 83.7 %copy-start.6 = (s32[32,1,816]{2,1,0:T(1,128)}, s32[32,1,816]{2,1,0:T(1,128)S(1)}, u32[]{:S(2)}) copy-start(s32[32,1,816]{2,1,0:T(1,128)S(1)} %all-to-all-done) | copy-start | bytes 313348
  529.2 6.0 copy-start.1
  529.2 1108.3 %all-to-all-start.1 = ((f32[32,816,500]{2,1,0:T(8,128)}), f32[32,816,500]{2,1,0:T(8,128)}, u32[]{:S(2)}, u32[]{:S(2)}) async-start(f32[32,816,500]{2,1,0:T(8,128)} %bitcast.44), calls=%async_computation.1 | async-start | bytes 106954752 | tf_op jit(solution)/shard_map/all_to_all | solution.py:34
  535.2 0.9 copy-start.3
  536.1 96.2 %copy-start.9 = (s32[32]{0:T(128)S(1)}, s32[32]{0:T(128)}, u32[]{:S(2)}) copy-start(s32[32]{0:T(128)} %copy-done.8) | copy-start | bytes 388
  536.1 187.2 %copy-start.12 = (s32[32]{0:T(128)S(1)}, s32[32]{0:T(128)}, u32[]{:S(2)}) copy-start(s32[32]{0:T(128)} %copy-done.11) | copy-start | bytes 388
  1878.7 26.7 copy-start.5
  1905.5 88.6 %copy-start.10 = (pred[32,816]{1,0:T(8,128)(4,1)S(1)}, pred[32,816]{1,0:T(8,128)(4,1)}, u32[]{:S(2)}) copy-start(pred[32,816]{1,0:T(8,128)(4,1)} %iota_compare_fusion) | copy-start | bytes 78340
  2029.8 77.3 %copy-start.7 = (s32[32,1,816]{2,1,0:T(1,128)S(1)}, s32[32,1,816]{2,1,0:T(1,128)}, u32[]{:S(2)}) copy-start(s32[32,1,816]{2,1,0:T(1,128)} %copy-done.6) | copy-start | bytes 313348
  2029.8 1275.3 %all-to-all-start.2 = ((f32[32,816,500]{2,1,0:T(8,128)}), f32[32,816,500]{2,1,0:T(8,128)}, u32[]{:S(2)}, u32[]{:S(2)}) async-start(f32[32,816,500]{2,1,0:T(8,128)} %broadcast_select_fusion), calls=%async_computation.2 | async-start | bytes 106954752 | tf_op jit(solution)/shard_map/all_to_all | solution.py:49
where the time goes:
time: 3520 us; the launch traced here: 3510 us
  blocking collectives  1200 us (34%)
  waiting for transfers between devices  914 us (26%)
  local copies, waits for them, and re-layouts  808 us (23%)
  other arithmetic  500 us (14%)
  starting transfers between devices  90.5 us (3%)
    psum x1, blocking collectives, device_step(): total_loss = lax.psum(local_loss, 'ep') / (n_pairs * group_size)  1200 us
    all_to_all x1, waiting for transfers between devices, device_step(): lax.all_to_all(served, 'ep', 0, 0).reshape(group_size * capacity, width)  914 us
    scatter-add x1, other arithmetic, device_step(): jax.ops.segment_sum(returned.reshape(group_size * capacity, width), incom...  170 us
    gather x2, local copies, waits for them, and re-layouts, device_step(): sort_order[jnp.minimum(owner_starts[:, None] + rank_ids[None, :], n_look...  134 us
    gather x2, local copies, waits for them, and re-layouts, device_step(): requests = jnp.where(filled, stack_row[source], 0).astype(jnp.int32)  134 us
    scatter-add x1, other arithmetic, device_step(): owner_counts = jnp.bincount(owners, length=group_size)  121 us
    gather x1, local copies, waits for them, and re-layouts, device_step(): owner_sorted = owners[sort_order]  96.2 us
    gather x1, local copies, waits for them, and re-layouts, device_step(): looked = fetched[slot_of]  89.7 us
  transfers between devices with their start and end apart: 3, of which 1 were waited for; matrix products, arithmetic and copies ran while one was open for 6% of the time, Pallas kernels for 0%

commit v1 on v0

v1 whole, which is shorter than its diff:
```python
import functools

import jax
import jax.numpy as jnp
from jax import lax
from jax.experimental import pallas as pl
from jax.experimental.pallas import tpu as pltpu
from jax.sharding import PartitionSpec as P

LEARN_RATE = 0.5
LANES = 128
SUB = 4
TAIL = 500 - 3 * LANES
CHUNK = 512
SLOTS = 1280
BATCH = 64
ANY = pl.ANY


def load_table(table, wide, stage, sems):
    rows = table.shape[0]
    n_chunks = rows // CHUNK

    def copy(k):
        return pltpu.make_async_copy(table.at[pl.ds(k * CHUNK, CHUNK)], stage.at[k % 2], sems.at[k % 2])

    copy(0).start()
    for k in range(n_chunks):
        if k + 1 < n_chunks:
            copy(k + 1).start()
        copy(k).wait()
        buf = stage.at[k % 2]

        @pl.loop(0, CHUNK // 32)
        def _(g):
            for i in range(4):
                r8 = pl.multiple_of((g * 4 + i) * 8, 8)
                w8 = pl.multiple_of((k * CHUNK + (g * 4 + i) * 8) * SUB, 32)
                for j in range(SUB):
                    if j < SUB - 1:
                        wide[pl.ds(w8 + j, 8, stride=SUB), :] = buf[pl.ds(r8, 8), j * LANES:(j + 1) * LANES]
                    else:
                        wide[pl.ds(w8 + j, 8, stride=SUB), :] = jnp.concatenate(
                            [buf[pl.ds(r8, 8), j * LANES:j * LANES + TAIL], jnp.zeros((8, LANES - TAIL), jnp.float32)],
                            axis=1)


def store_table(out, stage, sems, value):
    rows = out.shape[0]
    n_chunks = rows // CHUNK

    def copy(k):
        return pltpu.make_async_copy(stage.at[k % 2], out.at[pl.ds(k * CHUNK, CHUNK)], sems.at[k % 2])

    for k in range(n_chunks):
        if k >= 2:
            copy(k - 2).wait()
        buf = stage.at[k % 2]

        @pl.loop(0, CHUNK // 32)
        def _(g):
            for i in range(4):
                r8 = pl.multiple_of((g * 4 + i) * 8, 8)
                w8 = pl.multiple_of((k * CHUNK + (g * 4 + i) * 8) * SUB, 32)
                for j in range(SUB):
                    piece = value(w8, j)
                    if j < SUB - 1:
                        buf[pl.ds(r8, 8), j * LANES:(j + 1) * LANES] = piece
                    else:
                        buf[pl.ds(r8, 8), j * LANES:j * LANES + TAIL] = piece[:, :TAIL]

        copy(k).start()
    copy(n_chunks - 2).wait()
    copy(n_chunks - 1).wait()


def pick_kernel(rows4, table, out, wide, stage, sems):
    load_table(table, wide, stage, sems)

    @pl.loop(0, SLOTS // 16)
    def _(g):
        for i in range(16):
            k = g * 16 + i
            r4 = pl.multiple_of(rows4[k], SUB)
            out[pl.ds(pl.multiple_of(k * SUB, SUB), SUB), :] = wide[pl.ds(r4, SUB), :]


def pick_rows(rows4, table):
    return pl.pallas_call(
        pick_kernel,
        out_shape=jax.ShapeDtypeStruct((SLOTS * SUB, LANES), jnp.float32),
        grid_spec=pltpu.PrefetchScalarGridSpec(
            num_scalar_prefetch=1, grid=(1,),
            in_specs=[pl.BlockSpec(memory_space=ANY)],
            out_specs=pl.BlockSpec((SLOTS * SUB, LANES), lambda i, *_: (0, 0)),
            scratch_shapes=[pltpu.VMEM((table.shape[0] * SUB, LANES), jnp.float32),
                            pltpu.VMEM((2, CHUNK, table.shape[1]), jnp.float32),
                            pltpu.SemaphoreType.DMA((2,))]),
        name='pick_rows')(rows4, table)


def add_kernel(rows4, table, grads, out, wide, stage, sems):
    load_table(table, wide, stage, sems)

    @pl.loop(0, SLOTS // 16)
    def _(g):
        for i in range(16):
            k = g * 16 + i
            r4 = pl.multiple_of(rows4[k], SUB)
            wide[pl.ds(r4, SUB), :] = wide[pl.ds(r4, SUB), :] - LEARN_RATE * grads[pl.ds(pl.multiple_of(k * SUB, SUB), SUB), :]

    store_table(out, stage, sems, lambda w8, j: wide[pl.ds(w8 + j, 8, stride=SUB), :])


def add_rows(rows4, table, grads):
    return pl.pallas_call(
        add_kernel,
        out_shape=jax.ShapeDtypeStruct(table.shape, jnp.float32),
        grid_spec=pltpu.PrefetchScalarGridSpec(
            num_scalar_prefetch=1, grid=(1,),
            in_specs=[pl.BlockSpec(memory_space=ANY),
                      pl.BlockSpec((SLOTS * SUB, LANES), lambda i, *_: (0, 0))],
            out_specs=pl.BlockSpec(memory_space=ANY),
            scratch_shapes=[pltpu.VMEM((table.shape[0] * SUB, LANES), jnp.float32),
                            pltpu.VMEM((2, CHUNK, table.shape[1]), jnp.float32),
                            pltpu.SemaphoreType.DMA((2,))]),
        name='add_rows')(rows4, table, grads)


def score_kernel(separate, bounds, row4s, slot4s, signs, *refs):
    if separate:
        table, acc, u_blk, out, gu_blk, loss_blk, wide, grad, stage, sems, prods, sgn, coef = refs
    else:
        table, u_blk, out, gu_blk, loss_blk, wide, grad, stage, sems, prods, sgn, coef = refs
    step = pl.program_id(0)

    @pl.when(step == 0)
    def _():
        load_table(table, wide, stage, sems)
        loss_blk[...] = jnp.zeros_like(loss_blk)

        @pl.loop(0, grad.shape[0] // 256)
        def _(g):
            grad[pl.ds(pl.multiple_of(g * 256, 256), 256), :] = jnp.zeros((256, LANES), jnp.float32)

    @pl.loop(0, SLOTS * SUB // 256)
    def _(g):
        gu_blk[pl.ds(pl.multiple_of(g * 256, 256), 256), :] = jnp.zeros((256, LANES), jnp.float32)

    begin, end = bounds[step], bounds[step + 1]

    @pl.loop(0, (end - begin + BATCH - 1) // BATCH)
    def _(b):
        base = begin + b * BATCH
        for i in range(BATCH):
            r4 = pl.multiple_of(row4s[base + i], SUB)
            s4 = pl.multiple_of(slot4s[base + i], SUB)
            prods[i * SUB:(i + 1) * SUB, :] = u_blk[pl.ds(s4, SUB), :] * wide[pl.ds(r4, SUB), :]
            sgn[i:i + 1, :] = jnp.full((1, LANES), signs[base + i], jnp.float32)
        part = prods[pl.ds(0, BATCH, stride=SUB), :]
        for j in range(1, SUB):
            part = part + prods[pl.ds(j, BATCH, stride=SUB), :]
        total = jnp.sum(part, axis=1, keepdims=True)
        live = lax.broadcasted_iota(jnp.int32, (BATCH, LANES), 0) < end - base
        sign = jnp.where(live, sgn[...], 0.0)
        signed = sign * total
        small = jnp.exp(-jnp.abs(signed))
        loss = jnp.maximum(signed, 0.0) + jnp.log1p(small)
        loss_blk[...] += jnp.sum((jnp.abs(sign) * loss).reshape(BATCH // 8, 8, LANES), axis=0)
        gain = sign * jnp.where(signed >= 0, 1.0, small) / (1.0 + small)
        for j in range(SUB):
            coef[pl.ds(j, BATCH, stride=SUB), :] = gain
        for i in range(BATCH):
            r4 = pl.multiple_of(row4s[base + i], SUB)
            s4 = pl.multiple_of(slot4s[base + i], SUB)
            c = coef[i * SUB:(i + 1) * SUB, :]
            gu_blk[pl.ds(s4, SUB), :] += c * wide[pl.ds(r4, SUB), :]
            grad[pl.ds(r4, SUB), :] += c * u_blk[pl.ds(s4, SUB), :]

    @pl.when(step == pl.num_programs(0) - 1)
    def _():
        if separate:
            load_table(acc, wide, stage, sems)
        store_table(out, stage, sems,
                    lambda w8, j: wide[pl.ds(w8 + j, 8, stride=SUB), :] - LEARN_RATE * grad[pl.ds(w8 + j, 8, stride=SUB), :])


def score_rows(bounds, row4s, slot4s, signs, table, acc, u_all):
    separate = acc is not None
    n_blocks = u_all.shape[0] // (SLOTS * SUB)
    blk = pl.BlockSpec((SLOTS * SUB, LANES), lambda i, *_: (i, 0))
    tables = (table, acc) if separate else (table,)
    return pl.pallas_call(
        functools.partial(score_kernel, separate),
        out_shape=(jax.ShapeDtypeStruct(table.shape, jnp.float32),
                   jax.ShapeDtypeStruct(u_all.shape, jnp.float32),
                   jax.ShapeDtypeStruct((8, LANES), jnp.float32)),
        grid_spec=pltpu.PrefetchScalarGridSpec(
            num_scalar_prefetch=4, grid=(n_blocks,),
            in_specs=[pl.BlockSpec(memory_space=ANY)] * len(tables) + [blk],
            out_specs=(pl.BlockSpec(memory_space=ANY), blk,
                       pl.BlockSpec((8, LANES), lambda i, *_: (0, 0))),
            scratch_shapes=[pltpu.VMEM((table.shape[0] * SUB, LANES), jnp.float32),
                            pltpu.VMEM((table.shape[0] * SUB, LANES), jnp.float32),
                            pltpu.VMEM((2, CHUNK, table.shape[1]), jnp.float32),
                            pltpu.SemaphoreType.DMA((2,)),
                            pltpu.VMEM((BATCH * SUB, LANES), jnp.float32),
                            pltpu.VMEM((BATCH, LANES), jnp.float32),
                            pltpu.VMEM((BATCH * SUB, LANES), jnp.float32)]),
        compiler_params=pltpu.CompilerParams(vmem_limit_bytes=60 * 1024 * 1024),
        name='score_rows')(bounds, row4s, slot4s, signs, *tables, u_all)


def solution(mesh):
    group = mesh.shape['ep']

    def device_step(table_in, table_out, centers, contexts, negatives):
        rows_dev = table_in.shape[0]
        n_pairs, n_neg = negatives.shape
        n_ref = n_pairs * (n_neg + 1)
        capacity = (3 * n_pairs * (n_neg + 2)) // (2 * group)
        me = lax.axis_index('ep')
        ids = jnp.arange(group, dtype=jnp.int32)

        all_centers = lax.all_gather(centers, 'ep', axis=0, tiled=True)
        all_owner = all_centers % group
        counts = jnp.sum((all_owner.reshape(group, n_pairs)[:, None, :] == ids[None, :, None]).astype(jnp.int32), axis=2)
        totals = jnp.sum(counts, axis=0)
        before = jnp.sum(jnp.where(ids[:, None] < me, counts, 0), axis=0)
        owner_c = centers % group
        one_hot = (owner_c[:, None] == ids[None, :])
        tri = (jnp.arange(n_pairs)[:, None] > jnp.arange(n_pairs)[None, :]).astype(jnp.bfloat16)
        earlier = jnp.dot(tri, one_hot.astype(jnp.bfloat16), preferred_element_type=jnp.float32).astype(jnp.int32)
        rank = jnp.sum(jnp.where(one_hot, earlier + before[None, :], 0), axis=1)
        n_rounds = (jnp.max(totals) + SLOTS - 1) // SLOTS
        place = jnp.arange(group * n_pairs, dtype=jnp.int32)
        big = jnp.int32(2 ** 31 - 1)
        mine = jnp.where(all_owner == me, place * rows_dev + all_centers // group, big)
        my_rows4 = (lax.sort(mine) % rows_dev) * SUB
        my_rows4 = jnp.concatenate([my_rows4, jnp.zeros((SLOTS,), jnp.int32)])

        words = jnp.concatenate([contexts[:, None], negatives], axis=1)
        owner_o = words % group
        row_o = words // group
        is_ctx = (jnp.arange(n_neg + 1) == 0).astype(jnp.int32)[None, :]
        spare_rank = jnp.arange(capacity, dtype=jnp.int32)

        def one_round(turn, acc_in, acc_out):
            local = rank - turn * SLOTS
            inside = (local >= 0) & (local < SLOTS)
            slot = owner_c * SLOTS + local
            code = (slot[:, None] * rows_dev + row_o) * 2 + is_ctx
            dest = jnp.where(inside[:, None], owner_o, group)
            dest_count = jnp.sum((dest.reshape(1, n_ref) == ids[:, None]).astype(jnp.int32), axis=1)
            spare_dest = jnp.where(spare_rank[None, :] < capacity - dest_count[:, None], ids[:, None], group)
            keys = jnp.concatenate([dest.reshape(n_ref), spare_dest.reshape(group * capacity)])
            vals = jnp.concatenate([code.reshape(n_ref), jnp.full((group * capacity,), big)])
            _, vals = lax.sort((keys, vals), num_keys=1, is_stable=False)
            got = lax.all_to_all(vals[:group * capacity].reshape(group, capacity), 'ep', 0, 0)
            refs = lax.sort(got.reshape(group * capacity))
            edges = jnp.arange(group + 1, dtype=jnp.int32) * (SLOTS * rows_dev * 2)
            bounds = jnp.sum((refs[None, :] < edges[:, None]).astype(jnp.int32), axis=1)
            signs = jnp.where(refs % 2 == 1, -1.0, 1.0)
            row4s = (refs // 2) % rows_dev * SUB
            slot4s = (refs // (2 * rows_dev)) % SLOTS * SUB
            pad = jnp.zeros((BATCH,), jnp.int32)
            row4s = jnp.concatenate([row4s, pad])
            slot4s = jnp.concatenate([slot4s, pad])
            signs = jnp.concatenate([signs, jnp.zeros((BATCH,), jnp.float32)])

            rows4 = lax.dynamic_slice(my_rows4, (turn * SLOTS,), (SLOTS,))
            u_mine = pick_rows(rows4, table_in)
            u_all = lax.all_gather(u_mine, 'ep', axis=0, tiled=True)
            new_out, gu, loss = score_rows(bounds, row4s, slot4s, signs, table_out, acc_out, u_all)
            gu_mine = lax.psum_scatter(gu, 'ep', scatter_dimension=0, tiled=True)
            new_in = add_rows(rows4, acc_in, gu_mine)
            return new_in, new_out, jnp.sum(loss[:, 0])

        new_in, new_out, loss = one_round(jnp.int32(0), table_in, None)

        def more(state):
            return state[0] < n_rounds

        def again(state):
            turn, acc_in, acc_out, acc_loss = state
            acc_in, acc_out, part = one_round(turn, acc_in, acc_out)
            return turn + 1, acc_in, acc_out, acc_loss + part

        _, new_in, new_out, loss = lax.while_loop(more, again, (jnp.int32(1), new_in, new_out, loss))
        total_loss = lax.psum(loss, 'ep') / (n_pairs * group)
        return total_loss, new_in, new_out

    return jax.shard_map(device_step, mesh=mesh,
                         in_specs=(P('ep', None), P('ep', None), P('ep'), P('ep'), P('ep', None)),
                         out_specs=(P(), P('ep', None), P('ep', None)), check_vma=False)
```

time: 3520 us -> 1680 us (0.48)
  blocking collectives: 1200 us -> 92.3 us
  local copies, waits for them, and re-layouts: 808 us -> 52.1 us
  other arithmetic: 500 us -> 50.4 us
  waiting for transfers between devices: 914 us -> 1250 us
  Pallas kernels: 0 us -> 205 us
  starting transfers between devices: 90.5 us -> 2.66 us
    psum x1, blocking collectives: 1200 us -> 48.6 us  [device_step(): total_loss = lax.psum(loss, 'ep') / (n_pairs * group)]
    all_to_all x3 -> x1, waiting for transfers between devices: 914 us -> 0.47 us  [one_round(): lax.all_to_all(vals[:group * capacity].reshape(group, capacity), 'ep', 0, 0)]
    reduce_scatter x0 -> x1, waiting for transfers between devices: none -> 870 us  [one_round(): gu_mine = lax.psum_scatter(gu, 'ep', scatter_dimension=0, tiled=True)]
    gather x10 -> x0, local copies, waits for them, and re-layouts: 628 us -> none  [the longest x2 134 us: device_step(): sort_order[jnp.minimum(owner_starts[:, None] + rank_ids[None, :], n_look...]
    all_gather x0 -> x1, waiting for transfers between devices: none -> 379 us  [one_round(): u_all = lax.all_gather(u_mine, 'ep', axis=0, tiled=True)]
    scatter-add x2 -> x0, other arithmetic: 291 us -> none  [the longest x1 170 us: device_step(): jax.ops.segment_sum(returned.reshape(group_size * capacity, width), incom...]
    pallas_call x0 -> x3, Pallas kernels: none -> 205 us  [the longest x1 177 us: score_rows(): pl.pallas_call(functools.partial(score_kernel, separate), out_shape=(jax....]
    all_to_all x3 -> x1, starting transfers between devices: 90.5 us -> 2.57 us  [one_round(): lax.all_to_all(vals[:group * capacity].reshape(group, capacity), 'ep', 0, 0)]
  transfers between devices with their start and end apart: 3 -> 3, of which waited for: 1 -> 3; matrix products, arithmetic and copies ran while one was open for 6% -> 3% of each run, Pallas kernels for 0% -> 0%
where the time goes in v1:
time: 1680 us; the launch traced here: 1670 us
  waiting for transfers between devices  1250 us (74%)
  Pallas kernels  205 us (12%)
  blocking collectives  92.3 us (5%)
  local copies, waits for them, and re-layouts  52.1 us (3%)
  other arithmetic  50.4 us (3%)
  between operations  17.2 us (1%)
    reduce_scatter x1, waiting for transfers between devices, one_round(): gu_mine = lax.psum_scatter(gu, 'ep', scatter_dimension=0, tiled=True)  870 us
    all_gather x1, waiting for transfers between devices, one_round(): u_all = lax.all_gather(u_mine, 'ep', axis=0, tiled=True)  379 us
    pallas_call x1, Pallas kernels, score_rows(): pl.pallas_call(functools.partial(score_kernel, separate), out_shape=(jax....  177 us
    psum x1, blocking collectives, device_step(): total_loss = lax.psum(loss, 'ep') / (n_pairs * group)  48.6 us
    unnamed x14, local copies, waits for them, and re-layouts  47 us
    all_gather x1, blocking collectives, device_step(): all_centers = lax.all_gather(centers, 'ep', axis=0, tiled=True)  43.6 us
  transfers between devices with their start and end apart: 3, of which 3 were waited for; matrix products, arithmetic and copies ran while one was open for 3% of the time, Pallas kernels for 0%

profile of v1, /device:TPU:0, one launch (start us, length us, event | category | flops | bytes accessed | tf_op | source)
XLA Modules:
  0.0 1671.7 jit_solution(8259324050386459676)
XLA Ops:
  7.2 43.6 %all_gather.9 = s32[32768]{0:T(1024)S(1)} all-gather(s32[1024]{0:T(1024)} %param.9), channel_id=1, replica_groups=mesh['ep'=32] {'ep'}, dimensions={0}, use_global_device_ids=true | all-gather | bytes 135168 | tf_op jit(solution)/shard_map/all_gather | solution.py:225
  51.0 11.2 sort.84
  62.8 19.7 %copy.45.table = f32[4096,500]{1,0:T(8,128)} copy(f32[4096,500]{0,1:T(8,128)} %param.7) | data formatting | bytes 16384000 | tf_op args[0]
  82.5 10.0 pick_rows.6
  92.6 1.1 convert_reduce_fusion.2
  96.6 23.0 %sort.85 = (s32[42496]{0:T(1024)}, s32[42496]{0:T(1024)S(1)}) sort(s32[42496]{0:T(1024)S(1)} %pad_add_fusion.1, s32[42496]{0:T(1024)S(1)} %concatenate.45), dimensions={0}, to_apply=%region_5.6 | sort | flops 679936 | bytes 679936 | tf_op jit(solution)/shard_map/sort | solution.py:258
  119.7 0.8 all_to_all.16
  120.5 2.6 all-to-all-start.1
  123.2 9.2 copy.44.refs_0_
  133.2 11.1 sort.86
  144.6 0.6 concatenate.47.slot4s
  145.2 0.7 concatenate.46.row4s
  145.9 0.6 concatenate.48.signs
  146.6 1.2 convert_reduce_fusion.4.bounds
  147.8 378.7 %all-gather.3.cloned.1.call-done.refs_1_ = f32[163840,128]{1,0:T(8,128)} async-done(((f32[5120,128]{1,0:T(8,128)}), f32[163840,128]{1,0:T(8,128)}) %all-gather.3.cloned.1.call-update) | async-done | bytes 83886096 | tf_op jit(solution)/shard_map/all_gather | solution.py:273
  526.5 177.0 %score_rows.6 = (f32[4096,500]{1,0:T(8,128)}, f32[163840,128]{1,0:T(8,128)}, f32[8,128]{1,0:T(8,128)}) custom-call(s32[33]{0:T(128)} %convert_reduce_fusion.4.bounds, s32[26176]{0:T(1024)} %concatenate.46.row4s, s32[26176]{0:T(1024)} %concatenate.47.slot4s, f32[26176]{0:T(1024)} %concatenate.48.signs, f32[4096,500]{1,0:T(8,128)} %copy.44.refs_0_, ...), custom_call_target="tpu_custom_call" | custom-call | tf_op jit(solution)/shard_map/score_rows/pallas_call | solution.py:193
  703.6 0.6 reduce_max.9
  705.4 0.6 slice_reduce_fusion.1
  706.0 870.0 %reduce-scatter.3.cloned.1.call-done.grads = f32[5120,128]{1,0:T(8,128)} async-done(((f32[163840,128]{1,0:T(8,128)}), f32[5120,128]{1,0:T(8,128)}) %reduce-scatter.3.cloned.1.call-update) | async-done | bytes 2621456 | tf_op jit(solution)/shard_map/reduce_scatter | solution.py:275
  1575.9 18.3 %add_rows.6 = f32[4096,500]{1,0:T(8,128)} custom-call(s32[1280]{0:T(1024)} %dynamic_slice.9.rows4, f32[4096,500]{1,0:T(8,128)} %copy.45.table, f32[5120,128]{1,0:T(8,128)} %reduce-scatter.3.cloned.1.call-done.grads), custom_call_target="tpu_custom_call" | custom-call | tf_op jit(solution)/shard_map/add_rows/pallas_call | solution.py:116
  1594.3 2.0 while.19
  1596.3 48.6 %psum.7 = f32[]{:T(128)} all-reduce(f32[]{:T(128)} %get-tuple-element.272), channel_id=1, replica_groups=mesh['ep'=32] {'ep'}, use_global_device_ids=true, to_apply=%region_20.21 | all-reduce | flops 1 | bytes 8 | tf_op jit(solution)/shard_map/psum | solution.py:290
  1644.9 8.9 copy.50
  1653.8 8.9 copy.51
  (52 shorter events, 5.3 us)
Async XLA Ops:
  7.2 519.3 %all-gather.3.cloned.1.call-start = ((), (), s32[]{:S(2)}) async-start(), calls=%async_computation.4 | async-start | bytes 86507520 | tf_op jit(solution)/shard_map/all_gather | solution.py:273
  82.5 11.3 copy-start.2
  82.5 12.3 copy-start.1
  82.5 12.3 copy-start.3
  120.5 12.3 all-to-all-start.1
  123.1 1452.8 %reduce-scatter.3.cloned.1.call-start = ((), (), s32[]{:S(2)}) async-start(), calls=%async_computation.5 | async-start | bytes 86507520 | tf_op jit(solution)/shard_map/reduce_scatter | solution.py:275
  703.5 1.8 copy-start.4
Sparse Core Ops, SparseCore 0:
  92.7 433.7 all-gather.2
  703.7 872.1 reduce-scatter.2

commit v2 on v1

v2 whole, which is shorter than its diff:
```python
import functools

import jax
import jax.numpy as jnp
from jax import lax
from jax.experimental import pallas as pl
from jax.experimental.pallas import tpu as pltpu
from jax.sharding import PartitionSpec as P

LEARN_RATE = 0.5
LANES = 128
SUB = 4
TAIL = 500 - 3 * LANES
CHUNK = 512
SLOTS = 1248
BATCH = 64
ROOM = 768
LEFT = 32
ANY = pl.ANY
MESH = pl.DeviceIdType.MESH


def load_table(table, wide, stage, sems, first=0):
    rows = table.shape[0]
    n_chunks = rows // CHUNK

    def copy(k):
        return pltpu.make_async_copy(table.at[pl.ds(k * CHUNK, CHUNK)], stage.at[k % 2], sems.at[k % 2])

    copy(0).start()
    for k in range(n_chunks):
        if k + 1 < n_chunks:
            copy(k + 1).start()
        copy(k).wait()
        buf = stage.at[k % 2]

        @pl.loop(0, CHUNK // 32)
        def _(g):
            for i in range(4):
                r8 = pl.multiple_of((g * 4 + i) * 8, 8)
                w8 = pl.multiple_of((first + k * CHUNK + (g * 4 + i) * 8) * SUB, 32)
                for j in range(SUB):
                    if j < SUB - 1:
                        wide[pl.ds(w8 + j, 8, stride=SUB), :] = buf[pl.ds(r8, 8), j * LANES:(j + 1) * LANES]
                    else:
                        wide[pl.ds(w8 + j, 8, stride=SUB), :] = jnp.concatenate(
                            [buf[pl.ds(r8, 8), j * LANES:j * LANES + TAIL], jnp.zeros((8, LANES - TAIL), jnp.float32)],
                            axis=1)


def store_table(out, stage, sems, value):
    rows = out.shape[0]
    n_chunks = rows // CHUNK

    def copy(k):
        return pltpu.make_async_copy(stage.at[k % 2], out.at[pl.ds(k * CHUNK, CHUNK)], sems.at[k % 2])

    for k in range(n_chunks):
        if k >= 2:
            copy(k - 2).wait()
        buf = stage.at[k % 2]

        @pl.loop(0, CHUNK // 32)
        def _(g):
            for i in range(4):
                r8 = pl.multiple_of((g * 4 + i) * 8, 8)
                w8 = pl.multiple_of((k * CHUNK + (g * 4 + i) * 8) * SUB, 32)
                for j in range(SUB):
                    piece = value(w8, j)
                    if j < SUB - 1:
                        buf[pl.ds(r8, 8), j * LANES:(j + 1) * LANES] = piece
                    else:
                        buf[pl.ds(r8, 8), j * LANES:j * LANES + TAIL] = piece[:, :TAIL]

        copy(k).start()
    copy(n_chunks - 2).wait()
    copy(n_chunks - 1).wait()


def pick_kernel(rows4, table, out, wide, stage, sems):
    load_table(table, wide, stage, sems)

    @pl.loop(0, SLOTS // 16)
    def _(g):
        for i in range(16):
            k = g * 16 + i
            r4 = pl.multiple_of(rows4[k], SUB)
            out[pl.ds(pl.multiple_of(k * SUB, SUB), SUB), :] = wide[pl.ds(r4, SUB), :]


def pick_rows(rows4, table):
    return pl.pallas_call(
        pick_kernel,
        out_shape=jax.ShapeDtypeStruct((SLOTS * SUB, LANES), jnp.float32),
        grid_spec=pltpu.PrefetchScalarGridSpec(
            num_scalar_prefetch=1, grid=(1,),
            in_specs=[pl.BlockSpec(memory_space=ANY)],
            out_specs=pl.BlockSpec((SLOTS * SUB, LANES), lambda i, *_: (0, 0)),
            scratch_shapes=[pltpu.VMEM((table.shape[0] * SUB, LANES), jnp.float32),
                            pltpu.VMEM((2, CHUNK, table.shape[1]), jnp.float32),
                            pltpu.SemaphoreType.DMA((2,))]),
        name='pick_rows')(rows4, table)


def add_kernel(rows4, table, grads, out, wide, stage, sems):
    load_table(table, wide, stage, sems)

    @pl.loop(0, SLOTS // 16)
    def _(g):
        for i in range(16):
            k = g * 16 + i
            r4 = pl.multiple_of(rows4[k], SUB)
            wide[pl.ds(r4, SUB), :] = wide[pl.ds(r4, SUB), :] - LEARN_RATE * grads[pl.ds(pl.multiple_of(k * SUB, SUB), SUB), :]

    store_table(out, stage, sems, lambda w8, j: wide[pl.ds(w8 + j, 8, stride=SUB), :])


def add_rows(rows4, table, grads):
    return pl.pallas_call(
        add_kernel,
        out_shape=jax.ShapeDtypeStruct(table.shape, jnp.float32),
        grid_spec=pltpu.PrefetchScalarGridSpec(
            num_scalar_prefetch=1, grid=(1,),
            in_specs=[pl.BlockSpec(memory_space=ANY),
                      pl.BlockSpec((SLOTS * SUB, LANES), lambda i, *_: (0, 0))],
            out_specs=pl.BlockSpec(memory_space=ANY),
            scratch_shapes=[pltpu.VMEM((table.shape[0] * SUB, LANES), jnp.float32),
                            pltpu.VMEM((2, CHUNK, table.shape[1]), jnp.float32),
                            pltpu.SemaphoreType.DMA((2,))]),
        name='add_rows')(rows4, table, grads)


def score_kernel(bounds, row4s, slot4s, own, other, u_blk, own_grad, other_grad, gu_blk, loss_blk,
                 wide, grad, stage, sems, prods, flag, coef):
    step = pl.program_id(0)
    rows = own.shape[0]

    @pl.when(step == 0)
    def _():
        load_table(own, wide, stage, sems)
        load_table(other, wide, stage, sems, rows)
        loss_blk[...] = jnp.zeros_like(loss_blk)

        @pl.loop(0, grad.shape[0] // 256)
        def _(g):
            grad[pl.ds(pl.multiple_of(g * 256, 256), 256), :] = jnp.zeros((256, LANES), jnp.float32)

    @pl.loop(0, SLOTS * SUB // 128)
    def _(g):
        gu_blk[pl.ds(pl.multiple_of(g * 128, 128), 128), :] = jnp.zeros((128, LANES), jnp.float32)

    begin, end = bounds[step], bounds[step + 1]

    @pl.loop(0, (end - begin + BATCH - 1) // BATCH)
    def _(b):
        base = begin + b * BATCH
        for i in range(BATCH):
            r4 = pl.multiple_of(row4s[base + i], SUB)
            code = slot4s[base + i]
            ctx = code % 2
            s4 = pl.multiple_of(code - ctx, SUB)
            prods[i * SUB:(i + 1) * SUB, :] = u_blk[pl.ds(s4, SUB), :] * wide[pl.ds(r4, SUB), :]
            flag[i:i + 1, :] = jnp.full((1, LANES), ctx, jnp.int32)
        part = prods[pl.ds(0, BATCH, stride=SUB), :]
        for j in range(1, SUB):
            part = part + prods[pl.ds(j, BATCH, stride=SUB), :]
        total = jnp.sum(part, axis=1, keepdims=True)
        live = lax.broadcasted_iota(jnp.int32, (BATCH, LANES), 0) < end - base
        sign = jnp.where(live, jnp.where(flag[...] == 1, -1.0, 1.0), 0.0)
        signed = sign * total
        small = jnp.exp(-jnp.abs(signed))
        loss = jnp.maximum(signed, 0.0) + jnp.log1p(small)
        loss_blk[...] += jnp.sum((jnp.abs(sign) * loss).reshape(BATCH // 8, 8, LANES), axis=0)
        gain = sign * jnp.where(signed >= 0, 1.0, small) / (1.0 + small)
        for j in range(SUB):
            coef[pl.ds(j, BATCH, stride=SUB), :] = gain
        for i in range(BATCH):
            r4 = pl.multiple_of(row4s[base + i], SUB)
            code = slot4s[base + i]
            s4 = pl.multiple_of(code - code % 2, SUB)
            c = coef[i * SUB:(i + 1) * SUB, :]
            gu_blk[pl.ds(s4, SUB), :] += c * wide[pl.ds(r4, SUB), :]
            grad[pl.ds(r4, SUB), :] += c * u_blk[pl.ds(s4, SUB), :]

    @pl.when(step == pl.num_programs(0) - 1)
    def _():
        first = pltpu.make_async_copy(grad.at[pl.ds(0, rows * SUB)], own_grad, sems.at[0])
        second = pltpu.make_async_copy(grad.at[pl.ds(rows * SUB, rows * SUB)], other_grad, sems.at[1])
        first.start()
        second.start()
        first.wait()
        second.wait()


def score_rows(bounds, row4s, slot4s, own, other, u_all):
    rows, width = own.shape
    n_blocks = u_all.shape[0] // (SLOTS * SUB)
    blk = pl.BlockSpec((SLOTS * SUB, LANES), lambda i, *_: (i, 0))
    half = jax.ShapeDtypeStruct((rows * SUB, LANES), jnp.float32)
    return pl.pallas_call(
        score_kernel,
        out_shape=(half, half, jax.ShapeDtypeStruct(u_all.shape, jnp.float32),
                   jax.ShapeDtypeStruct((8, LANES), jnp.float32)),
        grid_spec=pltpu.PrefetchScalarGridSpec(
            num_scalar_prefetch=3, grid=(n_blocks,),
            in_specs=[pl.BlockSpec(memory_space=ANY), pl.BlockSpec(memory_space=ANY), blk],
            out_specs=(pl.BlockSpec(memory_space=ANY), pl.BlockSpec(memory_space=ANY), blk,
                       pl.BlockSpec((8, LANES), lambda i, *_: (0, 0))),
            scratch_shapes=[pltpu.VMEM((2 * rows * SUB, LANES), jnp.float32),
                            pltpu.VMEM((2 * rows * SUB, LANES), jnp.float32),
                            pltpu.VMEM((2, CHUNK, width), jnp.float32),
                            pltpu.SemaphoreType.DMA((2,)),
                            pltpu.VMEM((BATCH * SUB, LANES), jnp.float32),
                            pltpu.VMEM((BATCH, LANES), jnp.int32),
                            pltpu.VMEM((BATCH * SUB, LANES), jnp.float32)]),
        compiler_params=pltpu.CompilerParams(vmem_limit_bytes=60 * 1024 * 1024),
        name='score_rows')(bounds, row4s, slot4s, own, other, u_all)


def finish_kernel(table, first, second, out):
    @pl.loop(0, CHUNK // 32)
    def _(g):
        for i in range(4):
            r8 = pl.multiple_of((g * 4 + i) * 8, 8)
            w8 = pl.multiple_of((g * 4 + i) * 8 * SUB, 32)
            for j in range(SUB):
                cols = slice(j * LANES, (j + 1) * LANES if j < SUB - 1 else j * LANES + TAIL)
                grad = first[pl.ds(w8 + j, 8, stride=SUB), :] + second[pl.ds(w8 + j, 8, stride=SUB), :]
                if j == SUB - 1:
                    grad = grad[:, :TAIL]
                out[pl.ds(r8, 8), cols] = table[pl.ds(r8, 8), cols] - LEARN_RATE * grad


def finish_rows(table, first, second):
    rows, width = table.shape
    native = pl.BlockSpec((CHUNK, width), lambda i: (i, 0))
    wide = pl.BlockSpec((CHUNK * SUB, LANES), lambda i: (i, 0))
    return pl.pallas_call(
        finish_kernel, out_shape=jax.ShapeDtypeStruct(table.shape, jnp.float32), grid=(rows // CHUNK,),
        in_specs=[native, wide, wide], out_specs=native, name='finish_rows')(table, first, second)


def place_of():
    me = lax.axis_index('ep')
    x, y, z = (me // 2) % 2, (me // 4) % 2, me // 8
    return me, x, y, z, me + 2 - 4 * x, me + 4 - 8 * y


def plane_order(z):
    far = 3 * (1 - z // 2)
    near = 1 + z % 2
    return z, near, 6 - far - near - z, far


def meet_neighbours(me, z, x_peer, y_peer):
    barrier = pltpu.get_barrier_semaphore()
    pl.semaphore_signal(barrier, inc=1, device_id=(x_peer,), device_id_type=MESH)
    pl.semaphore_signal(barrier, inc=1, device_id=(y_peer,), device_id_type=MESH)

    @pl.when(z < 3)
    def _():
        pl.semaphore_signal(barrier, inc=1, device_id=(me + 8,), device_id_type=MESH)

    @pl.when(z > 0)
    def _():
        pl.semaphore_signal(barrier, inc=1, device_id=(me - 8,), device_id_type=MESH)

    @pl.when((z > 0) & (z < 3))
    def _():
        pl.semaphore_wait(barrier, 4)

    @pl.when((z == 0) | (z == 3))
    def _():
        pl.semaphore_wait(barrier, 3)


def remote(src, dst, send, recv, peer):
    return pltpu.make_async_remote_copy(src_ref=src, dst_ref=dst, send_sem=send, recv_sem=recv,
                                        device_id=(peer,), device_id_type=MESH)


def gather_kernel(mine, out, zs, zr, xs, xr, ys, yr, local_sem):
    me, x, y, z, x_peer, y_peer = place_of()
    half = mine.shape[0] // 2
    low, high = pl.ds(0, half), pl.ds(half, half)
    planes = plane_order(z)

    def up(p, src):
        return remote(src, out.at[p, y, x], zs.at[0, p], zr.at[0, p], me + 8)

    def down(p, src):
        return remote(src, out.at[p, y, x], zs.at[1, p], zr.at[1, p], me - 8)

    def held(p):
        return out.at[p, y, x]

    def to_x(k, m, src, row, part):
        return remote(src, out.at[planes[k], row, x, part], xs.at[m, k], xr.at[m, k], x_peer)

    def to_y(k, m, src, col, part):
        return remote(src, out.at[planes[k], y, col, part], ys.at[m, k], yr.at[m, k], y_peer)

    def own_pieces(k):
        src = mine if k == 0 else held(planes[k])
        return (to_y(k, 0, src.at[low], x, low), to_x(k, 0, src.at[high], y, high),
                to_y(k, 1, src.at[high], x, high), to_x(k, 1, src.at[low], y, low))

    def second_x(k):
        return to_x(k, 2, out.at[planes[k], 1 - y, x, low], 1 - y, low)

    def second_y(k):
        return to_y(k, 2, out.at[planes[k], y, 1 - x, high], 1 - x, high)

    def from_x(k, m, row, part):
        spot = out.at[planes[k], row, 1 - x, part]
        return remote(spot, spot, xs.at[m, k], xr.at[m, k], x_peer)

    def from_y(k, m, col, part):
        spot = out.at[planes[k], 1 - y, col, part]
        return remote(spot, spot, ys.at[m, k], yr.at[m, k], y_peer)

    meet_neighbours(me, z, x_peer, y_peer)
    keep = pltpu.make_async_copy(mine, out.at[z, y, x], local_sem)

    @pl.when(z < 3)
    def _():
        up(z, mine).start()

    @pl.when(z > 0)
    def _():
        down(z, mine).start()

    for piece in own_pieces(0):
        piece.start()
    keep.start()

    def relay(k):
        from_y(k, 0, x, low).wait_recv()
        second_x(k).start()
        from_x(k, 0, y, high).wait_recv()
        second_y(k).start()

    for k in range(1, 4):
        p = planes[k]

        @pl.when(p < z)
        def _():
            up(p, held(p)).wait_recv()

            @pl.when(z < 3)
            def _():
                up(p, held(p)).start()

        @pl.when(p > z)
        def _():
            down(p, held(p)).wait_recv()

            @pl.when(z > 0)
            def _():
                down(p, held(p)).start()

        for piece in own_pieces(k):
            piece.start()
        relay(k - 1)
    relay(3)

    keep.wait()
    for k in range(4):
        from_y(k, 1, x, high).wait_recv()
        from_x(k, 1, y, low).wait_recv()
        from_x(k, 2, 1 - y, low).wait_recv()
        from_y(k, 2, 1 - x, high).wait_recv()
        for piece in own_pieces(k):
            piece.wait_send()
        second_x(k).wait_send()
        second_y(k).wait_send()
        p = planes[k]

        @pl.when((p <= z) & (z < 3))
        def _():
            up(p, held(p)).wait_send()

        @pl.when((p >= z) & (z > 0))
        def _():
            down(p, held(p)).wait_send()


def gather_slots(mine):
    rows = mine.shape[0]
    dma = pltpu.SemaphoreType.DMA
    out = pl.pallas_call(
        gather_kernel,
        out_shape=jax.ShapeDtypeStruct((4, 2, 2, rows, LANES), jnp.float32),
        in_specs=[pl.BlockSpec(memory_space=pltpu.VMEM)],
        out_specs=pl.BlockSpec(memory_space=ANY),
        scratch_shapes=[dma((2, 4)), dma((2, 4)), dma((3, 4)), dma((3, 4)), dma((3, 4)), dma((3, 4)), dma],
        compiler_params=pltpu.CompilerParams(collective_id=1, has_side_effects=True),
        name='gather_slots')(mine)
    return out.reshape(16 * rows, LANES)


def scatter_kernel(parts, out, r1x, r1y, r2x, r2y, zu, zd, stage, zs, zr, xs, xr, ys, yr, stage_sem):
    me, x, y, z, x_peer, y_peer = place_of()
    half = out.shape[0] // 2
    low, high = pl.ds(0, half), pl.ds(half, half)
    planes = plane_order(z)[::-1]

    def x1(k, h):
        row = 1 - y if h == 0 else y
        return remote(parts.at[planes[k], row, 1 - x, low], r1x.at[k, h], xs.at[h, k], xr.at[h, k], x_peer)

    def y1(k, h):
        col = 1 - x if h == 0 else x
        return remote(parts.at[planes[k], 1 - y, col, high], r1y.at[k, h], ys.at[h, k], yr.at[h, k], y_peer)

    def x2(k):
        return remote(r1y.at[k, 0], r2y.at[k], xs.at[2, k], xr.at[2, k], x_peer)

    def y2(k):
        return remote(r1x.at[k, 0], r2x.at[k], ys.at[2, k], yr.at[2, k], y_peer)

    def load(k, i):
        p = planes[k]
        src = (parts.at[p, 1 - y, x, low], parts.at[p, y, x, low],
               parts.at[p, y, 1 - x, high], parts.at[p, y, x, high])[i]
        return pltpu.make_async_copy(src, stage.at[i], stage_sem.at[i])

    def add(dst, *others):
        @pl.loop(0, half // 64)
        def _(g):
            rows = pl.ds(pl.multiple_of(g * 64, 64), 64)
            value = dst[rows, :]
            for other in others:
                value = value + other[rows, :]
            dst[rows, :] = value

    def up(c, k, src):
        p = planes[k]
        return remote(src, zu.at[c, p - 1], zs.at[c, 0, p], zr.at[c, 0, p], me + 8)

    def down(c, k, src):
        p = planes[k]
        return remote(src, zd.at[c, p], zs.at[c, 1, p], zr.at[c, 1, p], me - 8)

    meet_neighbours(me, z, x_peer, y_peer)
    for i in range(4):
        load(0, i).start()
    for k in range(2):
        for h in range(2):
            x1(k, h).start()
            y1(k, h).start()

    def settle(c, k, total, first, i):
        p = planes[k]
        load(k, i).wait()
        add(total, first, stage.at[i])
        if k < 3:
            load(k + 1, i).start()

        @pl.when((p >= z) & (z > 0))
        def _():
            up(c, k, total).wait_recv()
            add(total, zu.at[c, p - 1])

        @pl.when((p <= z) & (z < 3))
        def _():
            down(c, k, total).wait_recv()
            add(total, zd.at[c, p])

    def move(c, k, total):
        p = planes[k]

        @pl.when(p > z)
        def _():
            up(c, k, total).start()

        @pl.when(p < z)
        def _():
            down(c, k, total).start()

    def finish(k):
        x1(k, 1).wait_recv()
        y2(k).wait_recv()
        settle(0, k, r2x.at[k], r1x.at[k, 1], 1)
        if k < 3:
            move(0, k, r2x.at[k])
        y1(k, 1).wait_recv()
        x2(k).wait_recv()
        settle(1, k, r2y.at[k], r1y.at[k, 1], 3)
        if k < 3:
            move(1, k, r2y.at[k])

    for k in range(4):
        x1(k, 0).wait_recv()
        load(k, 0).wait()
        add(r1x.at[k, 0], stage.at[0])
        y1(k, 0).wait_recv()
        load(k, 2).wait()
        add(r1y.at[k, 0], stage.at[2])
        if k < 3:
            load(k + 1, 0).start()
            load(k + 1, 2).start()
        y2(k).start()
        x2(k).start()
        if k + 2 < 4:
            for h in range(2):
                x1(k + 2, h).start()
                y1(k + 2, h).start()
        if k > 0:
            finish(k - 1)
    finish(3)

    @pl.loop(0, half // 64)
    def _(g):
        rows = pl.ds(pl.multiple_of(g * 64, 64), 64)
        out[rows, :] = r2x[3, rows, :]
        out[pl.ds(pl.multiple_of(half + g * 64, 64), 64), :] = r2y[3, rows, :]

    for k in range(4):
        for h in range(2):
            x1(k, h).wait_send()
            y1(k, h).wait_send()
        x2(k).wait_send()
        y2(k).wait_send()
        if k < 3:
            p = planes[k]
            for c, total in ((0, r2x.at[k]), (1, r2y.at[k])):
                @pl.when(p > z)
                def _():
                    up(c, k, total).wait_send()

                @pl.when(p < z)
                def _():
                    down(c, k, total).wait_send()


def scatter_slots(parts):
    rows = parts.shape[0] // 16
    dma = pltpu.SemaphoreType.DMA
    half = rows // 2
    f32 = jnp.float32
    return pl.pallas_call(
        scatter_kernel,
        out_shape=jax.ShapeDtypeStruct((rows, LANES), f32),
        in_specs=[pl.BlockSpec(memory_space=ANY)],
        out_specs=pl.BlockSpec(memory_space=pltpu.VMEM),
        scratch_shapes=[pltpu.VMEM((4, 2, half, LANES), f32), pltpu.VMEM((4, 2, half, LANES), f32),
                        pltpu.VMEM((4, half, LANES), f32), pltpu.VMEM((4, half, LANES), f32),
                        pltpu.VMEM((2, 3, half, LANES), f32), pltpu.VMEM((2, 3, half, LANES), f32),
                        pltpu.VMEM((4, half, LANES), f32),
                        dma((2, 2, 4)), dma((2, 2, 4)), dma((3, 4)), dma((3, 4)), dma((3, 4)), dma((3, 4)), dma((4,))],
        compiler_params=pltpu.CompilerParams(collective_id=2, has_side_effects=True,
                                             vmem_limit_bytes=62 * 1024 * 1024),
        name='scatter_slots')(parts.reshape(4, 2, 2, rows, LANES))


def solution(mesh):
    group = mesh.shape['ep']

    def device_step(table_in, table_out, centers, contexts, negatives):
        rows_dev, width = table_in.shape
        n_pairs, n_neg = negatives.shape
        n_ref = n_pairs * (n_neg + 1)
        me = lax.axis_index('ep')
        ids = jnp.arange(group, dtype=jnp.int32)
        partner = [(d, d + 1 - 2 * (d % 2)) for d in range(group)]
        other_out = lax.ppermute(table_out, 'ep', partner)

        all_centers = lax.all_gather(centers, 'ep', axis=0, tiled=True)
        all_owner = all_centers % group
        counts = jnp.sum((all_owner.reshape(group, n_pairs)[:, None, :] == ids[None, :, None]).astype(jnp.int32), axis=2)
        totals = jnp.sum(counts, axis=0)
        before = jnp.sum(jnp.where(ids[:, None] < me, counts, 0), axis=0)
        owner_c = centers % group
        one_hot = (owner_c[:, None] == ids[None, :])
        tri = (jnp.arange(n_pairs)[:, None] > jnp.arange(n_pairs)[None, :]).astype(jnp.bfloat16)
        earlier = jnp.dot(tri, one_hot.astype(jnp.bfloat16), preferred_element_type=jnp.float32).astype(jnp.int32)
        rank = jnp.sum(jnp.where(one_hot, earlier + before[None, :], 0), axis=1)
        place = jnp.arange(group * n_pairs, dtype=jnp.int32)
        big = jnp.int32(2 ** 31 - 1)
        mine = jnp.where(all_owner == me, place * rows_dev + all_centers // group, big)
        rows4 = (lax.sort(mine)[:SLOTS] % rows_dev) * SUB
        u_mine = pick_rows(rows4, table_in)

        words = jnp.concatenate([contexts[:, None], negatives], axis=1)
        owner_o = words % group
        core_u = (owner_c % 2)[:, None]
        row_o = words // group + (owner_o + core_u) % 2 * rows_dev
        is_ctx = (jnp.arange(n_neg + 1) == 0).astype(jnp.int32)[None, :]
        code = ((owner_c // 2 * SLOTS + rank)[:, None] * (2 * rows_dev) + row_o) * 2 + is_ctx
        fits = rank < SLOTS
        dest = jnp.where(fits[:, None], owner_o // 2 * 2 + core_u, group)
        dest_count = jnp.sum((dest.reshape(1, n_ref) == ids[:, None]).astype(jnp.int32), axis=1)
        roomy = jnp.max(dest_count) <= ROOM
        fits = fits & roomy
        dest = jnp.where(roomy, dest, group)
        dest_count = jnp.where(roomy, dest_count, 0)
        spare_dest = jnp.where(jnp.arange(ROOM)[None, :] < ROOM - dest_count[:, None], ids[:, None], group)
        keys = jnp.concatenate([dest.reshape(n_ref), spare_dest.reshape(group * ROOM)])
        vals = jnp.concatenate([code.reshape(n_ref), jnp.full((group * ROOM,), big)])
        _, vals = lax.sort((keys, vals), num_keys=1, is_stable=False)
        got = lax.all_to_all(vals[:group * ROOM].reshape(group, ROOM), 'ep', 0, 0)
        refs = lax.sort(got.reshape(group * ROOM))
        edges = jnp.arange(group // 2 + 1, dtype=jnp.int32) * (SLOTS * rows_dev * 4)
        bounds = jnp.sum((refs[None, :] < edges[:, None]).astype(jnp.int32), axis=1)
        pad = jnp.zeros((BATCH,), jnp.int32)
        row4s = jnp.concatenate([(refs // 2) % (2 * rows_dev) * SUB, pad])
        slot4s = jnp.concatenate([(refs // (4 * rows_dev)) % SLOTS * SUB + refs % 2, pad])

        u_all = gather_slots(u_mine)
        own_grad, other_grad, gu, loss = score_rows(bounds, row4s, slot4s, table_out, other_out, u_all)
        back_grad = lax.ppermute(other_grad, 'ep', partner)
        gu_mine = scatter_slots(gu)
        new_in = add_rows(rows4, table_in, gu_mine)
        new_out = finish_rows(table_out, own_grad, back_grad)
        loss = jnp.sum(loss[:, 0])
        overflow = jnp.sum(jnp.where(fits, 0, 1))
        sums = lax.psum(jnp.stack([loss, overflow.astype(jnp.float32)]), 'ep')

        def more(state):
            return state[0] < jnp.where(sums[1] > 0.5, n_pairs // LEFT, 0)

        def again(state):
            turn, acc_in, acc_out, acc_loss = state

            def cut(a):
                return lax.all_gather(lax.dynamic_slice_in_dim(a, turn * LEFT, LEFT), 'ep', axis=0, tiled=True)

            word = jnp.concatenate([cut(centers)[:, None], cut(words)], axis=1)
            left = cut(jnp.where(fits, 0, 1))[:, None] == 1
            held = word % group == me
            row = word // group
            found = jnp.concatenate([table_in[row[:, :1]], table_out[row[:, 1:]]], axis=1)
            found = lax.psum(jnp.where(held[:, :, None], found, 0.0), 'ep')
            u_vec, o_vec = found[:, 0], found[:, 1:]
            sign = jnp.where(is_ctx == 1, -1.0, 1.0)
            signed = sign * jnp.sum(u_vec[:, None, :] * o_vec, axis=-1)
            part = jnp.sum(jnp.where(left & (me == 0), -jax.nn.log_sigmoid(-signed), 0.0))
            gain = jnp.where(left, sign * jax.nn.sigmoid(signed), 0.0)
            goal = jnp.where(held & left, row, rows_dev)
            grad_u = jnp.sum(gain[:, :, None] * o_vec, axis=1)
            grad_o = gain[:, :, None] * u_vec[:, None, :]
            acc_in = acc_in.at[goal[:, 0]].add(-LEARN_RATE * grad_u, mode='drop')
            acc_out = acc_out.at[goal[:, 1:].reshape(-1)].add(-LEARN_RATE * grad_o.reshape(-1, width), mode='drop')
            return turn + 1, acc_in, acc_out, acc_loss + lax.psum(part, 'ep')

        _, new_in, new_out, total = lax.while_loop(more, again, (jnp.int32(0), new_in, new_out, sums[0]))
        return total / (n_pairs * group), new_in, new_out

    return jax.shard_map(device_step, mesh=mesh,
                         in_specs=(P('ep', None), P('ep', None), P('ep'), P('ep'), P('ep', None)),
                         out_specs=(P(), P('ep', None), P('ep', None)), check_vma=False)
```

time: 1680 us -> 1180 us (0.70)
  waiting for transfers between devices: 1250 us -> 0.01 us
  Pallas kernels: 205 us -> 951 us
    reduce_scatter x1 -> x0, waiting for transfers between devices: 870 us -> none  [one_round(): gu_mine = lax.psum_scatter(gu, 'ep', scatter_dimension=0, tiled=True)]
    pallas_call x1 -> x4, Pallas kernels: 177 us -> 922 us  [the longest x1 358 us: scatter_slots(): pl.pallas_call(scatter_kernel, out_shape=jax.ShapeDtypeStruct((rows, LANE...]
    all_gather x1 -> x0, waiting for transfers between devices: 379 us -> none  [one_round(): u_all = lax.all_gather(u_mine, 'ep', axis=0, tiled=True)]
    unnamed x14 -> x6, local copies, waits for them, and re-layouts: 47 us -> 35.7 us
  transfers between devices with their start and end apart: 3 -> 3, of which waited for: 3 -> 0; matrix products, arithmetic and copies ran while one was open for 3% -> 6% of each run, Pallas kernels for 0% -> 62%
where the time goes in v2:
time: 1180 us; the launch traced here: 1170 us
  Pallas kernels  951 us (81%)
  blocking collectives  93.4 us (8%)
  other arithmetic  50.7 us (4%)
  local copies, waits for them, and re-layouts  50 us (4%)
  between operations  16.9 us (1%)
    pallas_call x1, Pallas kernels, scatter_slots(): pl.pallas_call(scatter_kernel, out_shape=jax.ShapeDtypeStruct((rows, LANE...  358 us
    pallas_call x1, Pallas kernels, gather_slots(): pl.pallas_call(gather_kernel, out_shape=jax.ShapeDtypeStruct((4, 2, 2, ro...  337 us
    pallas_call x1, Pallas kernels, score_rows(): pl.pallas_call(score_kernel, out_shape=(half, half, jax.ShapeDtypeStruct(...  214 us
    all_gather x1, blocking collectives, device_step(): all_centers = lax.all_gather(centers, 'ep', axis=0, tiled=True)  48.2 us
    psum x1, blocking collectives, device_step(): sums = lax.psum(jnp.stack([loss, overflow.astype(jnp.float32)]), 'ep')  45.1 us
    unnamed x6, local copies, waits for them, and re-layouts  35.7 us
  transfers between devices with their start and end apart: 3, of which 0 were waited for; matrix products, arithmetic and copies ran while one was open for 6% of the time, Pallas kernels for 62%

profile of v2, /device:TPU:0, one launch (start us, length us, event | category | flops | bytes accessed | tf_op | source)
XLA Modules:
  0.0 1166.1 jit_solution(11677043001866357379)
XLA Ops:
  7.7 48.2 %all_gather.21 = s32[32768]{0:T(1024)S(1)} all-gather(s32[1024]{0:T(1024)} %param.9), channel_id=1, replica_groups=mesh['ep'=32] {'ep'}, dimensions={0}, use_global_device_ids=true | all-gather | bytes 135168 | tf_op jit(solution)/shard_map/all_gather | solution.py:569
  58.6 0.7 fusion.45
  60.4 0.9 pad_add_fusion.2
  63.5 19.4 %sort.44 = (s32[40960]{0:T(1024)}, s32[40960]{0:T(1024)S(1)}) sort(s32[40960]{0:T(1024)S(1)} %pad_add_fusion.1, s32[40960]{0:T(1024)S(1)} %concatenate.39), dimensions={0}, to_apply=%region_6.7 | sort | flops 655360 | bytes 655360 | tf_op jit(solution)/shard_map/sort | solution.py:601
  83.6 2.8 all-to-all-start
  86.3 11.2 sort.43
  98.1 9.0 copy.99.own.table
  107.1 9.0 copy.101.table
  116.1 9.8 pick_rows.1.mine
  125.9 337.1 %gather_slots.1 = f32[4,2,2,4992,128]{4,3,2,1,0:T(8,128)} custom-call(f32[4992,128]{1,0:T(8,128)} %pick_rows.1.mine), custom_call_target="tpu_custom_call" | custom-call | tf_op jit(solution)/shard_map/gather_slots/pallas_call | solution.py:391
  463.1 11.3 sort.45
  475.9 1.0 convert_reduce_fusion.1.bounds
  476.9 9.2 copy.100.other
  486.2 213.9 %score_rows.1 = (f32[16384,128]{1,0:T(8,128)}, f32[16384,128]{1,0:T(8,128)}, f32[79872,128]{1,0:T(8,128)}, f32[8,128]{1,0:T(8,128)}) custom-call(s32[17]{0:T(128)} %convert_reduce_fusion.1.bounds, s32[24640]{0:T(1024)} %concatenate.40.row4s, s32[24640]{0:T(1024)} %concatenate.41.slot4s, f32[4096,500]{1,0:T(8,128)} %copy.99.own.table, ...), custom_call_target="tpu_custom_call" | custom-call | tf_op jit(solution)/shard_map/score_rows/pallas_call | solution.py:200
  701.5 1.3 slice_reduce_fusion
  702.8 0.7 pad_maximum_fusion
  703.5 45.1 %psum.27 = f32[2]{0:T(128)S(1)} all-reduce(f32[2]{0:T(128)S(1)} %pad_maximum_fusion), channel_id=1, replica_groups=mesh['ep'=32] {'ep'}, use_global_device_ids=true, to_apply=%region_11.12 | all-reduce | flops 2 | bytes 16 | tf_op jit(solution)/shard_map/psum | solution.py:618
  748.7 358.3 %scatter_slots.1.grads = f32[4992,128]{1,0:T(8,128)} custom-call(f32[4,2,2,4992,128]{4,3,2,1,0:T(8,128)} %bitcast.54), custom_call_target="tpu_custom_call" | custom-call | tf_op jit(solution)/shard_map/scatter_slots/pallas_call | solution.py:542
  1107.0 18.3 %add_rows.1 = f32[4096,500]{1,0:T(8,128)} custom-call(s32[1248]{0:T(1024)} %fusion.41.rows4, f32[4096,500]{1,0:T(8,128)} %copy.101.table, f32[4992,128]{1,0:T(8,128)} %scatter_slots.1.grads), custom_call_target="tpu_custom_call" | custom-call | tf_op jit(solution)/shard_map/add_rows/pallas_call | solution.py:119
  1125.3 13.1 %finish_rows.1 = f32[4096,500]{1,0:T(8,128)} custom-call(f32[4096,500]{1,0:T(8,128)} %copy.99.own.table, f32[16384,128]{1,0:T(8,128)} %get-tuple-element.188.first, f32[16384,128]{1,0:T(8,128)} %collective-permute-done.1.second), custom_call_target="tpu_custom_call" | custom-call | tf_op jit(solution)/shard_map/finish_rows/pallas_call | solution.py:238
  1138.4 1.8 while.18
  1138.4 1.2 slice.91
  1140.3 8.9 copy.105
  1149.1 8.9 copy.106
  (44 shorter events, 9.3 us)
Async XLA Ops:
  7.2 469.8 %collective-permute-start = (f32[4096,500]{0,1:T(8,128)}, f32[4096,500]{0,1:T(8,128)}, u32[]{:S(2)}, u32[]{:S(2)}) collective-permute-start(f32[4096,500]{0,1:T(8,128)} %param.8), channel_id=1, source_target_pairs={{0,1},{1,0},{2,3},{3,2},{4,5},{5,4},{6,7},{7,6},{8,9},{9,8},{10,11... | collective-permute-start | bytes 24576008 | tf_op jit(solution)/shard_map/ppermute | solution.py:567
  83.6 379.5 %all-to-all-start = ((s32[32,1,768]{2,1,0:T(1,128)}), s32[32,1,768]{2,1,0:T(1,128)S(1)}, u32[]{:S(2)}, u32[]{:S(2)}) async-start(s32[32,1,768]{2,1,0:T(1,128)} %bitcast.1), calls=%async_computation | async-start | bytes 196608 | tf_op jit(solution)/shard_map/all_to_all | solution.py:602
  700.1 425.2 %collective-permute-start.1 = (f32[16384,128]{1,0:T(8,128)}, f32[16384,128]{1,0:T(8,128)}, u32[]{:S(2)}, u32[]{:S(2)}) collective-permute-start(f32[16384,128]{1,0:T(8,128)} %get-tuple-element.189), channel_id=1, source_target_pairs={{0,1},{1,0},{2,3},{3,2},{4,5},{5,4},{6,7},{7,6},{8,9},{9,8},{10,11... | collective-permute-start | bytes 25165832 | tf_op jit(solution)/shard_map/ppermute | solution.py:612
  748.6 358.4 %copy-start.7 = (f32[2]{0:T(128)}, f32[2]{0:T(128)S(1)}, u32[]{:S(2)}) copy-start(f32[2]{0:T(128)S(1)} %psum.27) | copy-start | bytes 28

commit v3 on v2

--- a/solution.py
+++ b/solution.py
@@ -14,6 +14,9 @@
 CHUNK = 512
 SLOTS = 1248
 BATCH = 64
+UNROLL = 16
+STEP = 64
+UP, DOWN, LATE = range(3)
 ROOM = 768
 LEFT = 32
 ANY = pl.ANY
@@ -131,7 +134,7 @@
 
 
 def score_kernel(bounds, row4s, slot4s, own, other, u_blk, own_grad, other_grad, gu_blk, loss_blk,
-                 wide, grad, stage, sems, prods, flag, coef):
+                 wide, grad, stage, sems, prods, coef):
     step = pl.program_id(0)
     rows = own.shape[0]
 
@@ -149,24 +152,28 @@
     def _(g):
         gu_blk[pl.ds(pl.multiple_of(g * 128, 128), 128), :] = jnp.zeros((128, LANES), jnp.float32)
 
-    begin, end = bounds[step], bounds[step + 1]
+    begin, middle, end = bounds[2 * step], bounds[2 * step + 1], bounds[2 * step + 2]
+
+    def spots(k):
+        return pl.ds(pl.multiple_of(row4s[k], SUB), SUB), pl.ds(pl.multiple_of(slot4s[k], SUB), SUB)
 
     @pl.loop(0, (end - begin + BATCH - 1) // BATCH)
     def _(b):
         base = begin + b * BATCH
-        for i in range(BATCH):
-            r4 = pl.multiple_of(row4s[base + i], SUB)
-            code = slot4s[base + i]
-            ctx = code % 2
-            s4 = pl.multiple_of(code - ctx, SUB)
-            prods[i * SUB:(i + 1) * SUB, :] = u_blk[pl.ds(s4, SUB), :] * wide[pl.ds(r4, SUB), :]
-            flag[i:i + 1, :] = jnp.full((1, LANES), ctx, jnp.int32)
+
+        @pl.loop(0, BATCH // UNROLL)
+        def _(g):
+            for i in range(UNROLL):
+                k = g * UNROLL + i
+                row, slot = spots(base + k)
+                prods[pl.ds(pl.multiple_of(k * SUB, SUB), SUB), :] = u_blk[slot, :] * wide[row, :]
+
         part = prods[pl.ds(0, BATCH, stride=SUB), :]
         for j in range(1, SUB):
             part = part + prods[pl.ds(j, BATCH, stride=SUB), :]
         total = jnp.sum(part, axis=1, keepdims=True)
-        live = lax.broadcasted_iota(jnp.int32, (BATCH, LANES), 0) < end - base
-        sign = jnp.where(live, jnp.where(flag[...] == 1, -1.0, 1.0), 0.0)
+        number = lax.broadcasted_iota(jnp.int32, (BATCH, LANES), 0)
+        sign = jnp.where(number < end - base, jnp.where(number < middle - base, 1.0, -1.0), 0.0)
         signed = sign * total
         small = jnp.exp(-jnp.abs(signed))
         loss = jnp.maximum(signed, 0.0) + jnp.log1p(small)
@@ -174,13 +181,25 @@
         gain = sign * jnp.where(signed >= 0, 1.0, small) / (1.0 + small)
         for j in range(SUB):
             coef[pl.ds(j, BATCH, stride=SUB), :] = gain
-        for i in range(BATCH):
-            r4 = pl.multiple_of(row4s[base + i], SUB)
-            code = slot4s[base + i]
-            s4 = pl.multiple_of(code - code % 2, SUB)
-            c = coef[i * SUB:(i + 1) * SUB, :]
-            gu_blk[pl.ds(s4, SUB), :] += c * wide[pl.ds(r4, SUB), :]
-            grad[pl.ds(r4, SUB), :] += c * u_blk[pl.ds(s4, SUB), :]
+
+        @pl.loop(0, BATCH // UNROLL)
+        def _(g):
+            for i in range(0, UNROLL, 2):
+                k = g * UNROLL + i
+                row_a, slot_a = spots(base + k)
+                row_b, slot_b = spots(base + k + 1)
+                c_a = coef[pl.ds(pl.multiple_of(k * SUB, SUB), SUB), :]
+                c_b = coef[pl.ds(pl.multiple_of((k + 1) * SUB, SUB), SUB), :]
+                gu_a, gu_b = c_a * wide[row_a, :], c_b * wide[row_b, :]
+                go_a, go_b = c_a * u_blk[slot_a, :], c_b * u_blk[slot_b, :]
+                gu_b = gu_b + jnp.where(slot4s[base + k] == slot4s[base + k + 1], gu_a, 0.0)
+                go_b = go_b + jnp.where(row4s[base + k] == row4s[base + k + 1], go_a, 0.0)
+                gu_a, gu_b = gu_a + gu_blk[slot_a, :], gu_b + gu_blk[slot_b, :]
+                go_a, go_b = go_a + grad[row_a, :], go_b + grad[row_b, :]
+                gu_blk[slot_a, :] = gu_a
+                grad[row_a, :] = go_a
+                gu_blk[slot_b, :] = gu_b
+                grad[row_b, :] = go_b
 
     @pl.when(step == pl.num_programs(0) - 1)
     def _():
@@ -211,7 +230,6 @@
                             pltpu.VMEM((2, CHUNK, width), jnp.float32),
                             pltpu.SemaphoreType.DMA((2,)),
                             pltpu.VMEM((BATCH * SUB, LANES), jnp.float32),
-                            pltpu.VMEM((BATCH, LANES), jnp.int32),
                             pltpu.VMEM((BATCH * SUB, LANES), jnp.float32)]),
         compiler_params=pltpu.CompilerParams(vmem_limit_bytes=60 * 1024 * 1024),
         name='score_rows')(bounds, row4s, slot4s, own, other, u_all)
@@ -243,7 +261,16 @@
 def place_of():
     me = lax.axis_index('ep')
     x, y, z = (me // 2) % 2, (me // 4) % 2, me // 8
-    return me, x, y, z, me + 2 - 4 * x, me + 4 - 8 * y
+    return me, x, y, z, 1 - x, 1 - y, me + 2 - 4 * x, me + 4 - 8 * y, z > 0, z < 3
+
+
+def block_of(g, base=0):
+    return pl.ds(pl.multiple_of(base + g * STEP, STEP), STEP)
+
+
+def pair(sends, recvs, k):
+    at = k if isinstance(k, tuple) else (k,)
+    return sends.at[at], recvs.at[at]
 
 
 def plane_order(z):
@@ -252,24 +279,24 @@
     return z, near, 6 - far - near - z, far
 
 
-def meet_neighbours(me, z, x_peer, y_peer):
+def meet_neighbours(me, x_peer, y_peer, below, above):
     barrier = pltpu.get_barrier_semaphore()
     pl.semaphore_signal(barrier, inc=1, device_id=(x_peer,), device_id_type=MESH)
     pl.semaphore_signal(barrier, inc=1, device_id=(y_peer,), device_id_type=MESH)
 
-    @pl.when(z < 3)
+    @pl.when(above)
     def _():
         pl.semaphore_signal(barrier, inc=1, device_id=(me + 8,), device_id_type=MESH)
 
-    @pl.when(z > 0)
+    @pl.when(below)
     def _():
         pl.semaphore_signal(barrier, inc=1, device_id=(me - 8,), device_id_type=MESH)
 
-    @pl.when((z > 0) & (z < 3))
+    @pl.when(below & above)
     def _():
         pl.semaphore_wait(barrier, 4)
 
-    @pl.when((z == 0) | (z == 3))
+    @pl.when(~(below & above))
     def _():
         pl.semaphore_wait(barrier, 3)
 
@@ -279,17 +306,32 @@
                                         device_id=(peer,), device_id_type=MESH)
 
 
-def gather_kernel(mine, out, zs, zr, xs, xr, ys, yr, local_sem):
-    me, x, y, z, x_peer, y_peer = place_of()
-    half = mine.shape[0] // 2
-    low, high = pl.ds(0, half), pl.ds(half, half)
+def shares(rows):
+    small = rows * 9 // 78 // STEP * STEP
+    return rows // 2 - small, small
+
+
+def gather_kernel(mine, out, zs, zr, xs, xr, ys, yr, gs, gr, local_sem):
+    me, x, y, z, far_x, far_y, x_peer, y_peer, below, above = place_of()
+    big, small = shares(mine.shape[0])
+    low, high, both = pl.ds(0, big), pl.ds(big, big), pl.ds(0, 2 * big)
+    late = pl.ds(2 * big, 2 * small)
+    late_x, late_y = pl.ds(2 * big, small), pl.ds(2 * big + small, small)
     planes = plane_order(z)
 
     def up(p, src):
-        return remote(src, out.at[p, y, x], zs.at[0, p], zr.at[0, p], me + 8)
+        return remote(src.at[both], out.at[p, y, x, both], zs.at[UP, p], zr.at[UP, p], me + 8)
 
     def down(p, src):
-        return remote(src, out.at[p, y, x], zs.at[1, p], zr.at[1, p], me - 8)
+        return remote(src.at[both], out.at[p, y, x, both], zs.at[DOWN, p], zr.at[DOWN, p], me - 8)
+
+    def late_up(p):
+        piece = out.at[p, :, :, late]
+        return remote(piece, piece, zs.at[2, p], zr.at[2, p], me + 8)
+
+    def late_down(p):
+        piece = out.at[p, :, :, late]
+        return remote(piece, piece, zs.at[3, p], zr.at[3, p], me - 8)
 
     def held(p):
         return out.at[p, y, x]
@@ -306,33 +348,54 @@
                 to_y(k, 1, src.at[high], x, high), to_x(k, 1, src.at[low], y, low))
 
     def second_x(k):
-        return to_x(k, 2, out.at[planes[k], 1 - y, x, low], 1 - y, low)
+        return to_x(k, 2, out.at[planes[k], far_y, x, low], far_y, low)
 
     def second_y(k):
-        return to_y(k, 2, out.at[planes[k], y, 1 - x, high], 1 - x, high)
+        return to_y(k, 2, out.at[planes[k], y, far_x, high], far_x, high)
 
     def from_x(k, m, row, part):
-        spot = out.at[planes[k], row, 1 - x, part]
+        spot = out.at[planes[k], row, far_x, part]
         return remote(spot, spot, xs.at[m, k], xr.at[m, k], x_peer)
 
     def from_y(k, m, col, part):
-        spot = out.at[planes[k], 1 - y, col, part]
+        spot = out.at[planes[k], far_y, col, part]
         return remote(spot, spot, ys.at[m, k], yr.at[m, k], y_peer)
 
-    meet_neighbours(me, z, x_peer, y_peer)
+    def late1_x():
+        return remote(mine.at[late_x], out.at[z, y, x, late_x], *pair(gs, gr, 0), x_peer)
+
+    def late1_y():
+        return remote(mine.at[late_y], out.at[z, y, x, late_y], *pair(gs, gr, 1), y_peer)
+
+    def late2_y():
+        piece = out.at[z, y, :, late_x]
+        return remote(piece, piece, *pair(gs, gr, 2), y_peer)
+
+    def late2_x():
+        piece = out.at[z, :, x, late_y]
+        return remote(piece, piece, *pair(gs, gr, 3), x_peer)
+
+    meet_neighbours(me, x_peer, y_peer, below, above)
     keep = pltpu.make_async_copy(mine, out.at[z, y, x], local_sem)
-
-    @pl.when(z < 3)
+    keep.start()
+    late1_x().start()
+    late1_y().start()
+
+    @pl.when(above)
     def _():
         up(z, mine).start()
 
-    @pl.when(z > 0)
+    @pl.when(below)
     def _():
         down(z, mine).start()
 
+    keep.wait()
+    late1_x().wait_recv()
+    late2_y().start()
+    late1_y().wait_recv()
+    late2_x().start()
     for piece in own_pieces(0):
         piece.start()
-    keep.start()
 
     def relay(k):
         from_y(k, 0, x, low).wait_recv()
@@ -340,6 +403,25 @@
         from_x(k, 0, y, high).wait_recv()
         second_y(k).start()
 
+    def late_pass(k):
+        p = planes[k]
+
+        @pl.when(p < z)
+        def _():
+            late_up(p).wait_recv()
+
+            @pl.when(above)
+            def _():
+                late_up(p).start()
+
+        @pl.when(p > z)
+        def _():
+            late_down(p).wait_recv()
+
+            @pl.when(below)
+            def _():
+                late_down(p).start()
+
     for k in range(1, 4):
         p = planes[k]
 
@@ -347,7 +429,7 @@
         def _():
             up(p, held(p)).wait_recv()
 
-            @pl.when(z < 3)
+            @pl.when(above)
             def _():
                 up(p, held(p)).start()
 
@@ -355,34 +437,51 @@
         def _():
             down(p, held(p)).wait_recv()
 
-            @pl.when(z > 0)
+            @pl.when(below)
             def _():
                 down(p, held(p)).start()
 
         for piece in own_pieces(k):
             piece.start()
         relay(k - 1)
+        if k == 1:
+            late2_y().wait_recv()
+            late2_x().wait_recv()
+
+            @pl.when(above)
+            def _():
+                late_up(z).start()
+
+            @pl.when(below)
+            def _():
+                late_down(z).start()
+        else:
+            late_pass(k - 1)
     relay(3)
-
-    keep.wait()
+    late_pass(3)
+
+    for piece in (late1_x(), late1_y(), late2_x(), late2_y()):
+        piece.wait_send()
     for k in range(4):
         from_y(k, 1, x, high).wait_recv()
         from_x(k, 1, y, low).wait_recv()
-        from_x(k, 2, 1 - y, low).wait_recv()
-        from_y(k, 2, 1 - x, high).wait_recv()
+        from_x(k, 2, far_y, low).wait_recv()
+        from_y(k, 2, far_x, high).wait_recv()
         for piece in own_pieces(k):
             piece.wait_send()
         second_x(k).wait_send()
         second_y(k).wait_send()
         p = planes[k]
 
-        @pl.when((p <= z) & (z < 3))
+        @pl.when((p <= z) & above)
         def _():
             up(p, held(p)).wait_send()
-
-        @pl.when((p >= z) & (z > 0))
+            late_up(p).wait_send()
+
+        @pl.when((p >= z) & below)
         def _():
             down(p, held(p)).wait_send()
+            late_down(p).wait_send()
 
 
 def gather_slots(mine):
@@ -393,42 +492,46 @@
         out_shape=jax.ShapeDtypeStruct((4, 2, 2, rows, LANES), jnp.float32),
         in_specs=[pl.BlockSpec(memory_space=pltpu.VMEM)],
         out_specs=pl.BlockSpec(memory_space=ANY),
-        scratch_shapes=[dma((2, 4)), dma((2, 4)), dma((3, 4)), dma((3, 4)), dma((3, 4)), dma((3, 4)), dma],
+        scratch_shapes=[dma((4, 4)), dma((4, 4)), *[dma((3, 4))] * 4,
+                        dma((4,)), dma((4,)), dma],
         compiler_params=pltpu.CompilerParams(collective_id=1, has_side_effects=True),
         name='gather_slots')(mine)
     return out.reshape(16 * rows, LANES)
 
 
-def scatter_kernel(parts, out, r1x, r1y, r2x, r2y, zu, zd, stage, zs, zr, xs, xr, ys, yr, stage_sem):
-    me, x, y, z, x_peer, y_peer = place_of()
-    half = out.shape[0] // 2
+def scatter_kernel(parts, out, r1x, r1y, r2x, r2y, zu, zd, stage, lu, ld, held, ly2, lx1, lx2, ly1,
+                   zs, zr, xs, xr, ys, yr, gs, gr, stage_sem, held_sem):
+    me, x, y, z, far_x, far_y, x_peer, y_peer, below, above = place_of()
+    half, small = shares(out.shape[0])
     low, high = pl.ds(0, half), pl.ds(half, half)
+    late = pl.ds(2 * half, 2 * small)
+    late_a, late_b = pl.ds(0, small), pl.ds(small, small)
     planes = plane_order(z)[::-1]
 
     def x1(k, h):
-        row = 1 - y if h == 0 else y
-        return remote(parts.at[planes[k], row, 1 - x, low], r1x.at[k, h], xs.at[h, k], xr.at[h, k], x_peer)
+        row = far_y if h == 0 else y
+        return remote(parts.at[planes[k], row, far_x, low], r1x.at[k, h], xs.at[h, k], xr.at[h, k], x_peer)
 
     def y1(k, h):
-        col = 1 - x if h == 0 else x
-        return remote(parts.at[planes[k], 1 - y, col, high], r1y.at[k, h], ys.at[h, k], yr.at[h, k], y_peer)
+        col = far_x if h == 0 else x
+        return remote(parts.at[planes[k], far_y, col, high], r1y.at[k, h], ys.at[h, k], yr.at[h, k], y_peer)
 
     def x2(k):
-        return remote(r1y.at[k, 0], r2y.at[k], xs.at[2, k], xr.at[2, k], x_peer)
+        return remote(r1y.at[k, 0], r2y.at[k], *pair(xs, xr, (LATE, k)), x_peer)
 
     def y2(k):
-        return remote(r1x.at[k, 0], r2x.at[k], ys.at[2, k], yr.at[2, k], y_peer)
+        return remote(r1x.at[k, 0], r2x.at[k], *pair(ys, yr, (LATE, k)), y_peer)
 
     def load(k, i):
         p = planes[k]
-        src = (parts.at[p, 1 - y, x, low], parts.at[p, y, x, low],
-               parts.at[p, y, 1 - x, high], parts.at[p, y, x, high])[i]
+        src = (parts.at[p, far_y, x, low], parts.at[p, y, x, low],
+               parts.at[p, y, far_x, high], parts.at[p, y, x, high])[i]
         return pltpu.make_async_copy(src, stage.at[i], stage_sem.at[i])
 
     def add(dst, *others):
-        @pl.loop(0, half // 64)
+        @pl.loop(0, half // STEP)
         def _(g):
-            rows = pl.ds(pl.multiple_of(g * 64, 64), 64)
+            rows = block_of(g)
             value = dst[rows, :]
             for other in others:
                 value = value + other[rows, :]
@@ -436,13 +539,93 @@
 
     def up(c, k, src):
         p = planes[k]
-        return remote(src, zu.at[c, p - 1], zs.at[c, 0, p], zr.at[c, 0, p], me + 8)
+        return remote(src, zu.at[c, p - 1], zs.at[c, UP, p], zr.at[c, UP, p], me + 8)
 
     def down(c, k, src):
         p = planes[k]
-        return remote(src, zd.at[c, p], zs.at[c, 1, p], zr.at[c, 1, p], me - 8)
-
-    meet_neighbours(me, z, x_peer, y_peer)
+        return remote(src, zd.at[c, p], zs.at[c, DOWN, p], zr.at[c, DOWN, p], me - 8)
+
+    def late_load(p):
+        return pltpu.make_async_copy(parts.at[p, :, :, late], held, held_sem)
+
+    def late_up(p, src):
+        return remote(src, lu.at[p - 1], zs.at[LATE, UP, p], zr.at[LATE, UP, p], me + 8)
+
+    def late_down(p, src):
+        return remote(src, ld.at[p], zs.at[LATE, DOWN, p], zr.at[LATE, DOWN, p], me - 8)
+
+    def late_add(dst, src):
+        @pl.loop(0, 2 * small // STEP)
+        def _(g):
+            rows = block_of(g)
+            for i in range(2):
+                for j in range(2):
+                    dst[i, j, rows, :] = dst[i, j, rows, :] + src[i, j, rows, :]
+
+    def small_add(dst, src):
+        @pl.loop(0, small // STEP)
+        def _(g):
+            rows = block_of(g)
+            dst[rows, :] = dst[rows, :] + src[rows, :]
+
+    def late_stage(k):
+        p = planes[k]
+        if k < 3:
+            @pl.when(below & above)
+            def _():
+                late_load(p).start()
+
+            @pl.when((p > z) & below)
+            def _():
+                late_up(p, lu.at[p - 1]).wait_recv()
+                late_load(p).wait()
+                late_add(lu.at[p - 1], held)
+                late_up(p, lu.at[p - 1]).start()
+
+            @pl.when((p < z) & above)
+            def _():
+                late_down(p, ld.at[p]).wait_recv()
+                late_load(p).wait()
+                late_add(ld.at[p], held)
+                late_down(p, ld.at[p]).start()
+        else:
+            late_load(p).start()
+            late_load(p).wait()
+
+            @pl.when(below)
+            def _():
+                late_up(p, lu.at[p - 1]).wait_recv()
+                late_add(held, lu.at[p - 1])
+
+            @pl.when(above)
+            def _():
+                late_down(p, ld.at[p]).wait_recv()
+                late_add(held, ld.at[p])
+
+    def late_y1():
+        return remote(held.at[far_y, :, late_a], ly1, *pair(gs, gr, 0), y_peer)
+
+    def late_x1():
+        return remote(held.at[:, far_x, late_b], lx1, *pair(gs, gr, 1), x_peer)
+
+    def late_x2():
+        return remote(ly1.at[far_x], lx2, *pair(gs, gr, 2), x_peer)
+
+    def late_y2():
+        return remote(lx1.at[far_y], ly2, *pair(gs, gr, 3), y_peer)
+
+    meet_neighbours(me, x_peer, y_peer, below, above)
+    for k in range(3):
+        p = planes[k]
+
+        @pl.when(~below)
+        def _():
+            late_up(p, parts.at[p, :, :, late]).start()
+
+        @pl.when(~above)
+        def _():
+            late_down(p, parts.at[p, :, :, late]).start()
+
     for i in range(4):
         load(0, i).start()
     for k in range(2):
@@ -457,12 +640,12 @@
         if k < 3:
             load(k + 1, i).start()
 
-        @pl.when((p >= z) & (z > 0))
+        @pl.when((p >= z) & below)
         def _():
             up(c, k, total).wait_recv()
             add(total, zu.at[c, p - 1])
 
-        @pl.when((p <= z) & (z < 3))
+        @pl.when((p <= z) & above)
         def _():
             down(c, k, total).wait_recv()
             add(total, zd.at[c, p])
@@ -508,13 +691,36 @@
                 y1(k + 2, h).start()
         if k > 0:
             finish(k - 1)
+            late_stage(k - 1)
+    late_stage(3)
+    late_y1().start()
+    late_x1().start()
     finish(3)
-
-    @pl.loop(0, half // 64)
+    late_y1().wait_recv()
+    late_x1().wait_recv()
+    for i in range(2):
+        small_add(ly1.at[i], held.at[y, i, late_a])
+        small_add(lx1.at[i], held.at[i, x, late_b])
+
+    @pl.loop(0, half // STEP)
     def _(g):
-        rows = pl.ds(pl.multiple_of(g * 64, 64), 64)
+        rows = block_of(g)
         out[rows, :] = r2x[3, rows, :]
-        out[pl.ds(pl.multiple_of(half + g * 64, 64), 64), :] = r2y[3, rows, :]
+        out[block_of(g, half), :] = r2y[3, rows, :]
+
+    late_x2().start()
+    late_y2().start()
+    late_x2().wait_recv()
+    late_y2().wait_recv()
+
+    @pl.loop(0, small // STEP)
+    def _(g):
+        rows = block_of(g)
+        out[block_of(g, 2 * half), :] = ly1[x, rows, :] + lx2[rows, :]
+        out[block_of(g, 2 * half + small), :] = lx1[y, rows, :] + ly2[rows, :]
+
+    for piece in (late_x1(), late_y1(), late_x2(), late_y2()):
+        piece.wait_send()
 
     for k in range(4):
         for h in range(2):
@@ -524,6 +730,15 @@
         y2(k).wait_send()
         if k < 3:
             p = planes[k]
+
+            @pl.when(p > z)
+            def _():
+                late_up(p, lu.at[p - 1]).wait_send()
+
+            @pl.when(p < z)
+            def _():
+                late_down(p, ld.at[p]).wait_send()
+
             for c, total in ((0, r2x.at[k]), (1, r2y.at[k])):
                 @pl.when(p > z)
                 def _():
@@ -537,20 +752,22 @@
 def scatter_slots(parts):
     rows = parts.shape[0] // 16
     dma = pltpu.SemaphoreType.DMA
-    half = rows // 2
+    half, small = shares(rows)
     f32 = jnp.float32
     return pl.pallas_call(
         scatter_kernel,
         out_shape=jax.ShapeDtypeStruct((rows, LANES), f32),
         in_specs=[pl.BlockSpec(memory_space=ANY)],
         out_specs=pl.BlockSpec(memory_space=pltpu.VMEM),
-        scratch_shapes=[pltpu.VMEM((4, 2, half, LANES), f32), pltpu.VMEM((4, 2, half, LANES), f32),
-                        pltpu.VMEM((4, half, LANES), f32), pltpu.VMEM((4, half, LANES), f32),
-                        pltpu.VMEM((2, 3, half, LANES), f32), pltpu.VMEM((2, 3, half, LANES), f32),
-                        pltpu.VMEM((4, half, LANES), f32),
-                        dma((2, 2, 4)), dma((2, 2, 4)), dma((3, 4)), dma((3, 4)), dma((3, 4)), dma((3, 4)), dma((4,))],
+        scratch_shapes=[*[pltpu.VMEM((4, 2, half, LANES), f32)] * 2, *[pltpu.VMEM((4, half, LANES), f32)] * 2,
+                        *[pltpu.VMEM((2, 3, half, LANES), f32)] * 2, pltpu.VMEM((4, half, LANES), f32),
+                        *[pltpu.VMEM((3, 2, 2, 2 * small, LANES), f32)] * 2,
+                        pltpu.VMEM((2, 2, 2 * small, LANES), f32),
+                        *[pltpu.VMEM((small, LANES), f32), pltpu.VMEM((2, small, LANES), f32)] * 2,
+                        *[dma((3, 2, 4))] * 2, *[dma((3, 4))] * 4,
+                        *[dma((4,))] * 3, dma],
         compiler_params=pltpu.CompilerParams(collective_id=2, has_side_effects=True,
-                                             vmem_limit_bytes=62 * 1024 * 1024),
+                                             vmem_limit_bytes=63 * 1024 * 1024),
         name='scatter_slots')(parts.reshape(4, 2, 2, rows, LANES))
 
 
@@ -566,7 +783,7 @@
         partner = [(d, d + 1 - 2 * (d % 2)) for d in range(group)]
         other_out = lax.ppermute(table_out, 'ep', partner)
 
-        all_centers = lax.all_gather(centers, 'ep', axis=0, tiled=True)
+        all_centers = lax.all_to_all(jnp.broadcast_to(centers[None], (group, n_pairs)), 'ep', 0, 0).reshape(-1)
         all_owner = all_centers % group
         counts = jnp.sum((all_owner.reshape(group, n_pairs)[:, None, :] == ids[None, :, None]).astype(jnp.int32), axis=2)
         totals = jnp.sum(counts, axis=0)
@@ -579,7 +796,7 @@
         place = jnp.arange(group * n_pairs, dtype=jnp.int32)
         big = jnp.int32(2 ** 31 - 1)
         mine = jnp.where(all_owner == me, place * rows_dev + all_centers // group, big)
-        rows4 = (lax.sort(mine)[:SLOTS] % rows_dev) * SUB
+        rows4 = (lax.sort(mine, is_stable=False)[:SLOTS] % rows_dev) * SUB
         u_mine = pick_rows(rows4, table_in)
 
         words = jnp.concatenate([contexts[:, None], negatives], axis=1)
@@ -587,7 +804,8 @@
         core_u = (owner_c % 2)[:, None]
         row_o = words // group + (owner_o + core_u) % 2 * rows_dev
         is_ctx = (jnp.arange(n_neg + 1) == 0).astype(jnp.int32)[None, :]
-        code = ((owner_c // 2 * SLOTS + rank)[:, None] * (2 * rows_dev) + row_o) * 2 + is_ctx
+        block = (owner_c // 2)[:, None] * 2 + is_ctx
+        code = (block * SLOTS + rank[:, None]) * (2 * rows_dev) + row_o
         fits = rank < SLOTS
         dest = jnp.where(fits[:, None], owner_o // 2 * 2 + core_u, group)
         dest_count = jnp.sum((dest.reshape(1, n_ref) == ids[:, None]).astype(jnp.int32), axis=1)
@@ -600,12 +818,12 @@
         vals = jnp.concatenate([code.reshape(n_ref), jnp.full((group * ROOM,), big)])
         _, vals = lax.sort((keys, vals), num_keys=1, is_stable=False)
         got = lax.all_to_all(vals[:group * ROOM].reshape(group, ROOM), 'ep', 0, 0)
-        refs = lax.sort(got.reshape(group * ROOM))
-        edges = jnp.arange(group // 2 + 1, dtype=jnp.int32) * (SLOTS * rows_dev * 4)
+        refs = lax.sort(got.reshape(group * ROOM), is_stable=False)
+        edges = jnp.arange(group + 1, dtype=jnp.int32) * (SLOTS * rows_dev * 2)
         bounds = jnp.sum((refs[None, :] < edges[:, None]).astype(jnp.int32), axis=1)
         pad = jnp.zeros((BATCH,), jnp.int32)
-        row4s = jnp.concatenate([(refs // 2) % (2 * rows_dev) * SUB, pad])
-        slot4s = jnp.concatenate([(refs // (4 * rows_dev)) % SLOTS * SUB + refs % 2, pad])
+        row4s = jnp.concatenate([refs % (2 * rows_dev) * SUB, pad])
+        slot4s = jnp.concatenate([refs // (2 * rows_dev) % SLOTS * SUB, pad])
 
         u_all = gather_slots(u_mine)
         own_grad, other_grad, gu, loss = score_rows(bounds, row4s, slot4s, table_out, other_out, u_all)
@@ -614,8 +832,9 @@
         new_in = add_rows(rows4, table_in, gu_mine)
         new_out = finish_rows(table_out, own_grad, back_grad)
         loss = jnp.sum(loss[:, 0])
-        overflow = jnp.sum(jnp.where(fits, 0, 1))
-        sums = lax.psum(jnp.stack([loss, overflow.astype(jnp.float32)]), 'ep')
+        overflow = jnp.sum((~fits).astype(jnp.int32))
+        both = jnp.where(jnp.arange(LANES) == 0, loss, overflow.astype(jnp.float32))
+        sums = jnp.sum(lax.all_to_all(jnp.broadcast_to(both[None], (group, LANES)), 'ep', 0, 0), axis=0)
 
         def more(state):
             return state[0] < jnp.where(sums[1] > 0.5, n_pairs // LEFT, 0)
@@ -627,7 +846,7 @@
                 return lax.all_gather(lax.dynamic_slice_in_dim(a, turn * LEFT, LEFT), 'ep', axis=0, tiled=True)
 
             word = jnp.concatenate([cut(centers)[:, None], cut(words)], axis=1)
-            left = cut(jnp.where(fits, 0, 1))[:, None] == 1
+            left = cut((~fits).astype(jnp.int32))[:, None] == 1
             held = word % group == me
             row = word // group
             found = jnp.concatenate([table_in[row[:, :1]], table_out[row[:, 1:]]], axis=1)

time: 1180 us -> 1040 us (0.88)
  the two profiles are of different devices: /device:TPU:0 before, /device:TPU:16 now
where the time goes in v3:
time: 1040 us; the launch traced here: 1030 us
  Pallas kernels  862 us (83%)
  starting transfers between devices  57.5 us (6%)
  local copies, waits for them, and re-layouts  51.6 us (5%)
  other arithmetic  43.6 us (4%)
  between operations  17.2 us (2%)
    pallas_call x1, Pallas kernels, scatter_slots(): pl.pallas_call(scatter_kernel, out_shape=jax.ShapeDtypeStruct((rows, LANE...  390 us
    pallas_call x1, Pallas kernels, gather_slots(): pl.pallas_call(gather_kernel, out_shape=jax.ShapeDtypeStruct((4, 2, 2, ro...  283 us
    pallas_call x1, Pallas kernels, score_rows(): pl.pallas_call(score_kernel, out_shape=(half, half, jax.ShapeDtypeStruct(...  148 us
    all_to_all x1, starting transfers between devices, device_step(): lax.all_to_all(jnp.broadcast_to(both[None], (group, LANES)), 'ep', 0, 0)  41.1 us
    unnamed x7, local copies, waits for them, and re-layouts  35.7 us
  transfers between devices with their start and end apart: 5, of which 0 were waited for; matrix products, arithmetic and copies ran while one was open for 7% of the time, Pallas kernels for 68%

profile of v3, /device:TPU:16, one launch (start us, length us, event | category | flops | bytes accessed | tf_op | source)
XLA Modules:
  0.0 1033.1 jit_solution(4301242747918185052)
XLA Ops:
  7.2 1.4 broadcast_in_dim.179
  8.7 6.0 all-to-all-start
  14.7 0.9 pad_add_fusion.2
  16.3 9.0 copy.139.own.table
  26.1 9.0 copy.141.table
  35.2 7.3 sort.29
  47.1 19.1 %sort.30 = (s32[40960]{0:T(1024)}, s32[40960]{0:T(1024)S(1)}) sort(s32[40960]{0:T(1024)S(1)} %pad_add_fusion.1, s32[40960]{0:T(1024)S(1)} %concatenate.39), dimensions={0}, to_apply=%region_6.7 | sort | flops 655360 | bytes 655360 | tf_op jit(solution)/shard_map/sort | solution.py:819
  66.8 5.8 all-to-all-start.1
  73.3 9.8 pick_rows.1.mine
  83.1 283.0 %gather_slots.1 = f32[4,2,2,4992,128]{4,3,2,1,0:T(8,128)} custom-call(f32[4992,128]{1,0:T(8,128)} %pick_rows.1.mine), custom_call_target="tpu_custom_call" | custom-call | tf_op jit(solution)/shard_map/gather_slots/pallas_call | solution.py:490
  366.1 8.6 sort.31
  376.2 1.2 convert_reduce_fusion.1.bounds
  377.4 9.0 copy.140.other
  386.4 147.6 %score_rows.1 = (f32[16384,128]{1,0:T(8,128)}, f32[16384,128]{1,0:T(8,128)}, f32[79872,128]{1,0:T(8,128)}, f32[8,128]{1,0:T(8,128)}) custom-call(s32[33]{0:T(128)} %convert_reduce_fusion.1.bounds, s32[24640]{0:T(1024)} %concatenate.40.row4s, s32[24640]{0:T(1024)} %concatenate.41.slot4s, f32[4096,500]{1,0:T(8,128)} %copy.139.own.table, ...), custom_call_target="tpu_custom_call" | custom-call | tf_op jit(solution)/shard_map/score_rows/pallas_call | solution.py:219
  534.0 4.5 collective-permute-start.1
  539.7 1.3 slice_reduce_fusion
  542.3 41.1 %all-to-all-start.2 = ((f32[32,1,128]{2,1,0:T(1,128)}), f32[32,1,128]{2,1,0:T(1,128)S(1)}, u32[]{:S(2)}, u32[]{:S(2)}) async-start(f32[32,1,128]{2,1,0:T(1,128)} %broadcast_in_dim.192), calls=%async_computation.2 | async-start | bytes 32768 | tf_op jit(solution)/shard_map/all_to_all | solution.py:837
  583.4 390.0 %scatter_slots.1.grads = f32[4992,128]{1,0:T(8,128)} custom-call(f32[4,2,2,4992,128]{4,3,2,1,0:T(8,128)} %bitcast.57), custom_call_target="tpu_custom_call" | custom-call | tf_op jit(solution)/shard_map/scatter_slots/pallas_call | solution.py:757
  973.4 18.5 %add_rows.1 = f32[4096,500]{1,0:T(8,128)} custom-call(s32[1248]{0:T(1024)} %fusion.38.rows4, f32[4096,500]{1,0:T(8,128)} %copy.141.table, f32[4992,128]{1,0:T(8,128)} %scatter_slots.1.grads), custom_call_target="tpu_custom_call" | custom-call | tf_op jit(solution)/shard_map/add_rows/pallas_call | solution.py:122
  992.0 13.1 %finish_rows.1 = f32[4096,500]{1,0:T(8,128)} custom-call(f32[4096,500]{1,0:T(8,128)} %copy.139.own.table, f32[16384,128]{1,0:T(8,128)} %get-tuple-element.184.first, f32[16384,128]{1,0:T(8,128)} %collective-permute-done.1.second), custom_call_target="tpu_custom_call" | custom-call | tf_op jit(solution)/shard_map/finish_rows/pallas_call | solution.py:256
  1005.1 1.9 while.18
  1005.1 1.2 slice.92
  1007.0 8.9 copy.146
  1015.9 8.9 copy.147
  (46 shorter events, 10.1 us)
Async XLA Ops:
  7.2 370.2 %collective-permute-start = (f32[4096,500]{0,1:T(8,128)}, f32[4096,500]{0,1:T(8,128)}, u32[]{:S(2)}, u32[]{:S(2)}) collective-permute-start(f32[4096,500]{0,1:T(8,128)} %param.8), channel_id=1, source_target_pairs={{0,1},{1,0},{2,3},{3,2},{4,5},{5,4},{6,7},{7,6},{8,9},{9,8},{10,11... | collective-permute-start | bytes 24576008 | tf_op jit(solution)/shard_map/ppermute | solution.py:784
  8.7 26.4 %all-to-all-start = ((s32[32,1,1024]{2,1,0:T(1,128)}), s32[32,1,1024]{2,1,0:T(1,128)S(1)}, u32[]{:S(2)}, u32[]{:S(2)}) async-start(s32[32,1,1024]{2,1,0:T(1,128)} %broadcast_in_dim.179), calls=%async_computation | async-start | bytes 262144 | tf_op jit(solution)/shard_map/all_to_all | solution.py:786
  66.8 299.3 %all-to-all-start.1 = ((s32[32,1,768]{2,1,0:T(1,128)}), s32[32,1,768]{2,1,0:T(1,128)S(1)}, u32[]{:S(2)}, u32[]{:S(2)}) async-start(s32[32,1,768]{2,1,0:T(1,128)} %bitcast.2), calls=%async_computation.1 | async-start | bytes 196608 | tf_op jit(solution)/shard_map/all_to_all | solution.py:820
  534.0 458.0 %collective-permute-start.1 = (f32[16384,128]{1,0:T(8,128)}, f32[16384,128]{1,0:T(8,128)}, u32[]{:S(2)}, u32[]{:S(2)}) collective-permute-start(f32[16384,128]{1,0:T(8,128)} %get-tuple-element.185), channel_id=1, source_target_pairs={{0,1},{1,0},{2,3},{3,2},{4,5},{5,4},{6,7},{7,6},{8,9},{9,8},{10,11... | collective-permute-start | bytes 25165832 | tf_op jit(solution)/shard_map/ppermute | solution.py:830
  542.3 449.6 %all-to-all-start.2 = ((f32[32,1,128]{2,1,0:T(1,128)}), f32[32,1,128]{2,1,0:T(1,128)S(1)}, u32[]{:S(2)}, u32[]{:S(2)}) async-start(f32[32,1,128]{2,1,0:T(1,128)} %broadcast_in_dim.192), calls=%async_computation.2 | async-start | bytes 32768 | tf_op jit(solution)/shard_map/all_to_all | solution.py:837
  991.9 13.2 %copy-start.7 = (f32[128]{0:T(128)}, f32[128]{0:T(128)S(1)}, u32[]{:S(2)}) copy-start(f32[128]{0:T(128)S(1)} %reduce_sum.117) | copy-start | bytes 1540

commit v4 on v3

--- a/solution.py
+++ b/solution.py
@@ -17,6 +17,8 @@
 UNROLL = 16
 STEP = 64
 UP, DOWN, LATE = range(3)
+GATHER_PLAN = 'I0P0Z0Q0Z1P1R0J0Z2R1P2Z3P3Q1G0Q2G1R3Q3R2G2G3'
+SCATTER_PLAN = 'O0N0N2E0L0A0N1N3E1O1L2F0E2A1A2O2L1L3F1O3A3F2M0F3'
 ROOM = 768
 LEFT = 32
 ANY = pl.ANY
@@ -264,6 +266,11 @@
     return me, x, y, z, 1 - x, 1 - y, me + 2 - 4 * x, me + 4 - 8 * y, z > 0, z < 3
 
 
+def follow(plan, steps):
+    for name, plane in zip(plan[::2], plan[1::2]):
+        steps[name](int(plane))
+
+
 def block_of(g, base=0):
     return pl.ds(pl.multiple_of(base + g * STEP, STEP), STEP)
 
@@ -307,7 +314,7 @@
 
 
 def shares(rows):
-    small = rows * 9 // 78 // STEP * STEP
+    small = rows * 4 // 39 // STEP * STEP
     return rows // 2 - small, small
 
 
@@ -378,24 +385,47 @@
     meet_neighbours(me, x_peer, y_peer, below, above)
     keep = pltpu.make_async_copy(mine, out.at[z, y, x], local_sem)
     keep.start()
-    late1_x().start()
-    late1_y().start()
-
-    @pl.when(above)
-    def _():
-        up(z, mine).start()
-
-    @pl.when(below)
-    def _():
-        down(z, mine).start()
-
-    keep.wait()
-    late1_x().wait_recv()
-    late2_y().start()
-    late1_y().wait_recv()
-    late2_x().start()
-    for piece in own_pieces(0):
-        piece.start()
+
+    def late_out(k):
+        late1_x().start()
+        late1_y().start()
+
+    def late_on(k):
+        keep.wait()
+        late1_x().wait_recv()
+        late2_y().start()
+        late1_y().wait_recv()
+        late2_x().start()
+
+    def along_z(k):
+        p = planes[k]
+        src = mine if k == 0 else held(p)
+
+        @pl.when(p <= z)
+        def _():
+            if k > 0:
+                up(p, src).wait_recv()
+
+            @pl.when(above)
+            def _():
+                up(p, src).start()
+
+        @pl.when(p >= z)
+        def _():
+            if k > 0:
+                down(p, src).wait_recv()
+
+            @pl.when(below)
+            def _():
+                down(p, src).start()
+
+    def early_pieces(k):
+        for piece in own_pieces(k)[:2]:
+            piece.start()
+
+    def other_pieces(k):
+        for piece in own_pieces(k)[2:]:
+            piece.start()
 
     def relay(k):
         from_y(k, 0, x, low).wait_recv()
@@ -403,63 +433,32 @@
         from_x(k, 0, y, high).wait_recv()
         second_y(k).start()
 
-    def late_pass(k):
-        p = planes[k]
-
-        @pl.when(p < z)
-        def _():
-            late_up(p).wait_recv()
-
-            @pl.when(above)
-            def _():
-                late_up(p).start()
-
-        @pl.when(p > z)
-        def _():
-            late_down(p).wait_recv()
-
-            @pl.when(below)
-            def _():
-                late_down(p).start()
-
-    for k in range(1, 4):
-        p = planes[k]
-
-        @pl.when(p < z)
-        def _():
-            up(p, held(p)).wait_recv()
-
-            @pl.when(above)
-            def _():
-                up(p, held(p)).start()
-
-        @pl.when(p > z)
-        def _():
-            down(p, held(p)).wait_recv()
-
-            @pl.when(below)
-            def _():
-                down(p, held(p)).start()
-
-        for piece in own_pieces(k):
-            piece.start()
-        relay(k - 1)
-        if k == 1:
+    def late_along_z(k):
+        p = planes[k]
+        if k == 0:
             late2_y().wait_recv()
             late2_x().wait_recv()
 
+        @pl.when(p <= z)
+        def _():
+            if k > 0:
+                late_up(p).wait_recv()
+
             @pl.when(above)
             def _():
-                late_up(z).start()
+                late_up(p).start()
+
+        @pl.when(p >= z)
+        def _():
+            if k > 0:
+                late_down(p).wait_recv()
 
             @pl.when(below)
             def _():
-                late_down(z).start()
-        else:
-            late_pass(k - 1)
-    relay(3)
-    late_pass(3)
-
+                late_down(p).start()
+
+    follow(GATHER_PLAN, {'I': late_out, 'J': late_on, 'Z': along_z, 'P': early_pieces, 'Q': other_pieces,
+                         'R': relay, 'G': late_along_z})
     for piece in (late1_x(), late1_y(), late2_x(), late2_y()):
         piece.wait_send()
     for k in range(4):
@@ -602,6 +601,9 @@
                 late_down(p, ld.at[p]).wait_recv()
                 late_add(held, ld.at[p])
 
+            late_y1().start()
+            late_x1().start()
+
     def late_y1():
         return remote(held.at[far_y, :, late_a], ly1, *pair(gs, gr, 0), y_peer)
 
@@ -615,23 +617,8 @@
         return remote(lx1.at[far_y], ly2, *pair(gs, gr, 3), y_peer)
 
     meet_neighbours(me, x_peer, y_peer, below, above)
-    for k in range(3):
-        p = planes[k]
-
-        @pl.when(~below)
-        def _():
-            late_up(p, parts.at[p, :, :, late]).start()
-
-        @pl.when(~above)
-        def _():
-            late_down(p, parts.at[p, :, :, late]).start()
-
     for i in range(4):
         load(0, i).start()
-    for k in range(2):
-        for h in range(2):
-            x1(k, h).start()
-            y1(k, h).start()
 
     def settle(c, k, total, first, i):
         p = planes[k]
@@ -673,7 +660,26 @@
         if k < 3:
             move(1, k, r2y.at[k])
 
-    for k in range(4):
+    def late_ends(k):
+        p = planes[k]
+
+        @pl.when(~below)
+        def _():
+            late_up(p, parts.at[p, :, :, late]).start()
+
+        @pl.when(~above)
+        def _():
+            late_down(p, parts.at[p, :, :, late]).start()
+
+    def first_pieces(k):
+        x1(k, 0).start()
+        y1(k, 0).start()
+
+    def other_pieces(k):
+        x1(k, 1).start()
+        y1(k, 1).start()
+
+    def turn_corner(k):
         x1(k, 0).wait_recv()
         load(k, 0).wait()
         add(r1x.at[k, 0], stage.at[0])
@@ -685,22 +691,18 @@
             load(k + 1, 2).start()
         y2(k).start()
         x2(k).start()
-        if k + 2 < 4:
-            for h in range(2):
-                x1(k + 2, h).start()
-                y1(k + 2, h).start()
-        if k > 0:
-            finish(k - 1)
-            late_stage(k - 1)
-    late_stage(3)
-    late_y1().start()
-    late_x1().start()
-    finish(3)
-    late_y1().wait_recv()
-    late_x1().wait_recv()
-    for i in range(2):
-        small_add(ly1.at[i], held.at[y, i, late_a])
-        small_add(lx1.at[i], held.at[i, x, late_b])
+
+    def late_corner(k):
+        late_y1().wait_recv()
+        late_x1().wait_recv()
+        for i in range(2):
+            small_add(ly1.at[i], held.at[y, i, late_a])
+            small_add(lx1.at[i], held.at[i, x, late_b])
+        late_x2().start()
+        late_y2().start()
+
+    follow(SCATTER_PLAN, {'E': late_ends, 'N': first_pieces, 'O': other_pieces, 'A': turn_corner, 'F': finish,
+                          'L': late_stage, 'M': late_corner})
 
     @pl.loop(0, half // STEP)
     def _(g):
@@ -708,8 +710,6 @@
         out[rows, :] = r2x[3, rows, :]
         out[block_of(g, half), :] = r2y[3, rows, :]
 
-    late_x2().start()
-    late_y2().start()
     late_x2().wait_recv()
     late_y2().wait_recv()
 

time: 1040 us -> 911 us (0.88)
  the two profiles are of different devices: /device:TPU:16 before, /device:TPU:0 now
where the time goes in v4:
time: 911 us; the launch traced here: 901 us
  Pallas kernels  763 us (84%)
  local copies, waits for them, and re-layouts  51.6 us (6%)
  other arithmetic  43.6 us (5%)
  starting transfers between devices  24.6 us (3%)
  between operations  17.2 us (2%)
    pallas_call x1, Pallas kernels, scatter_slots(): pl.pallas_call(scatter_kernel, out_shape=jax.ShapeDtypeStruct((rows, LANE...  285 us
    pallas_call x1, Pallas kernels, gather_slots(): pl.pallas_call(gather_kernel, out_shape=jax.ShapeDtypeStruct((4, 2, 2, ro...  285 us
    pallas_call x1, Pallas kernels, score_rows(): pl.pallas_call(score_kernel, out_shape=(half, half, jax.ShapeDtypeStruct(...  152 us
    unnamed x7, local copies, waits for them, and re-layouts  35.7 us
    sort x1, other arithmetic, device_step(): _, vals = lax.sort((keys, vals), num_keys=1, is_stable=False)  19.1 us
    pallas_call x1, Pallas kernels, add_rows(): pl.pallas_call(add_kernel, out_shape=jax.ShapeDtypeStruct(table.shape, jn...  18.5 us
  transfers between devices with their start and end apart: 5, of which 0 were waited for; matrix products, arithmetic and copies ran while one was open for 8% of the time, Pallas kernels for 66%

profile of v4, /device:TPU:0, one launch (start us, length us, event | category | flops | bytes accessed | tf_op | source)
XLA Modules:
  0.0 901.4 jit_solution(8933158864028451525)
XLA Ops:
  7.7 1.4 broadcast_in_dim.179
  9.2 7.0 all-to-all-start
  16.1 0.9 pad_add_fusion.2
  17.0 0.7 fusion.40
  17.7 9.0 copy.139.own.table
  27.5 9.0 copy.141.table
  36.7 7.3 sort.29
  48.5 19.1 %sort.30 = (s32[40960]{0:T(1024)}, s32[40960]{0:T(1024)S(1)}) sort(s32[40960]{0:T(1024)S(1)} %pad_add_fusion.1, s32[40960]{0:T(1024)S(1)} %concatenate.39), dimensions={0}, to_apply=%region_6.7 | sort | flops 655360 | bytes 655360 | tf_op jit(solution)/shard_map/sort | solution.py:819
  68.3 5.8 all-to-all-start.1
  74.7 9.8 %pick_rows.1.mine = f32[4992,128]{1,0:T(8,128)} custom-call(s32[1248]{0:T(1024)} %fusion.38.rows4, f32[4096,500]{1,0:T(8,128)} %copy.141.table), custom_call_target="tpu_custom_call" | custom-call | tf_op jit(solution)/shard_map/pick_rows/pallas_call | solution.py:97
  84.5 284.5 %gather_slots.1 = f32[4,2,2,4992,128]{4,3,2,1,0:T(8,128)} custom-call(f32[4992,128]{1,0:T(8,128)} %pick_rows.1.mine), custom_call_target="tpu_custom_call" | custom-call | tf_op jit(solution)/shard_map/gather_slots/pallas_call | solution.py:489
  369.1 8.6 sort.31
  379.1 1.2 convert_reduce_fusion.1.bounds
  380.3 9.0 copy.140.other
  389.3 152.3 %score_rows.1 = (f32[16384,128]{1,0:T(8,128)}, f32[16384,128]{1,0:T(8,128)}, f32[79872,128]{1,0:T(8,128)}, f32[8,128]{1,0:T(8,128)}) custom-call(s32[33]{0:T(128)} %convert_reduce_fusion.1.bounds, s32[24640]{0:T(1024)} %concatenate.40.row4s, s32[24640]{0:T(1024)} %concatenate.41.slot4s, f32[4096,500]{1,0:T(8,128)} %copy.139.own.table, ...), custom_call_target="tpu_custom_call" | custom-call | tf_op jit(solution)/shard_map/score_rows/pallas_call | solution.py:221
  542.9 1.3 slice_reduce_fusion
  545.5 11.2 %all-to-all-start.2 = ((f32[32,1,128]{2,1,0:T(1,128)}), f32[32,1,128]{2,1,0:T(1,128)S(1)}, u32[]{:S(2)}, u32[]{:S(2)}) async-start(f32[32,1,128]{2,1,0:T(1,128)} %broadcast_in_dim.192), calls=%async_computation.2 | async-start | bytes 32768 | tf_op jit(solution)/shard_map/all_to_all | solution.py:837
  556.7 285.0 %scatter_slots.1.grads = f32[4992,128]{1,0:T(8,128)} custom-call(f32[4,2,2,4992,128]{4,3,2,1,0:T(8,128)} %bitcast.57), custom_call_target="tpu_custom_call" | custom-call | tf_op jit(solution)/shard_map/scatter_slots/pallas_call | solution.py:757
  841.7 18.5 %add_rows.1 = f32[4096,500]{1,0:T(8,128)} custom-call(s32[1248]{0:T(1024)} %fusion.38.rows4, f32[4096,500]{1,0:T(8,128)} %copy.141.table, f32[4992,128]{1,0:T(8,128)} %scatter_slots.1.grads), custom_call_target="tpu_custom_call" | custom-call | tf_op jit(solution)/shard_map/add_rows/pallas_call | solution.py:124
  860.2 13.1 %finish_rows.1 = f32[4096,500]{1,0:T(8,128)} custom-call(f32[4096,500]{1,0:T(8,128)} %copy.139.own.table, f32[16384,128]{1,0:T(8,128)} %get-tuple-element.184.first, f32[16384,128]{1,0:T(8,128)} %collective-permute-done.1.second), custom_call_target="tpu_custom_call" | custom-call | tf_op jit(solution)/shard_map/finish_rows/pallas_call | solution.py:258
  873.4 1.9 while.18
  873.4 1.2 slice.92
  875.3 8.9 copy.146
  884.2 8.9 copy.147
  (46 shorter events, 10.0 us)
Async XLA Ops:
  7.2 373.1 %collective-permute-start = (f32[4096,500]{0,1:T(8,128)}, f32[4096,500]{0,1:T(8,128)}, u32[]{:S(2)}, u32[]{:S(2)}) collective-permute-start(f32[4096,500]{0,1:T(8,128)} %param.8), channel_id=1, source_target_pairs={{0,1},{1,0},{2,3},{3,2},{4,5},{5,4},{6,7},{7,6},{8,9},{9,8},{10,11... | collective-permute-start | bytes 24576008 | tf_op jit(solution)/shard_map/ppermute | solution.py:784
  9.2 27.3 %all-to-all-start = ((s32[32,1,1024]{2,1,0:T(1,128)}), s32[32,1,1024]{2,1,0:T(1,128)S(1)}, u32[]{:S(2)}, u32[]{:S(2)}) async-start(s32[32,1,1024]{2,1,0:T(1,128)} %broadcast_in_dim.179), calls=%async_computation | async-start | bytes 262144 | tf_op jit(solution)/shard_map/all_to_all | solution.py:786
  68.3 300.8 %all-to-all-start.1 = ((s32[32,1,768]{2,1,0:T(1,128)}), s32[32,1,768]{2,1,0:T(1,128)S(1)}, u32[]{:S(2)}, u32[]{:S(2)}) async-start(s32[32,1,768]{2,1,0:T(1,128)} %bitcast.2), calls=%async_computation.1 | async-start | bytes 196608 | tf_op jit(solution)/shard_map/all_to_all | solution.py:820
  541.6 318.7 %collective-permute-start.1 = (f32[16384,128]{1,0:T(8,128)}, f32[16384,128]{1,0:T(8,128)}, u32[]{:S(2)}, u32[]{:S(2)}) collective-permute-start(f32[16384,128]{1,0:T(8,128)} %get-tuple-element.185), channel_id=1, source_target_pairs={{0,1},{1,0},{2,3},{3,2},{4,5},{5,4},{6,7},{7,6},{8,9},{9,8},{10,11... | collective-permute-start | bytes 25165832 | tf_op jit(solution)/shard_map/ppermute | solution.py:830
  545.5 314.7 %all-to-all-start.2 = ((f32[32,1,128]{2,1,0:T(1,128)}), f32[32,1,128]{2,1,0:T(1,128)S(1)}, u32[]{:S(2)}, u32[]{:S(2)}) async-start(f32[32,1,128]{2,1,0:T(1,128)} %broadcast_in_dim.192), calls=%async_computation.2 | async-start | bytes 32768 | tf_op jit(solution)/shard_map/all_to_all | solution.py:837
  860.2 13.2 %copy-start.7 = (f32[128]{0:T(128)}, f32[128]{0:T(128)S(1)}, u32[]{:S(2)}) copy-start(f32[128]{0:T(128)S(1)} %reduce_sum.117) | copy-start | bytes 1540

commit v5 on v4

--- a/solution.py
+++ b/solution.py
@@ -9,6 +9,7 @@
 
 LEARN_RATE = 0.5
 LANES = 128
+TILE = 8
 SUB = 4
 TAIL = 500 - 3 * LANES
 CHUNK = 512
@@ -16,16 +17,18 @@
 BATCH = 64
 UNROLL = 16
 STEP = 64
+COLS = 256
+TURNS = 4
 UP, DOWN, LATE = range(3)
-GATHER_PLAN = 'I0P0Z0Q0Z1P1R0J0Z2R1P2Z3P3Q1G0Q2G1R3Q3R2G2G3'
-SCATTER_PLAN = 'O0N0N2E0L0A0N1N3E1O1L2F0E2A1A2O2L1L3F1O3A3F2M0F3'
+GATHER_PLAN = 'Z0P0Q0I0X0R0Z1J0P1X1Z2G0P2Q2X2Q1R2Z3P3G1X3X4Q3G2R1R3X5X6X7G3'
+SCATTER_PLAN = 'O0N0N2E0A0E1N3N1L0X0O1L2X1F0E2L1A1A2F1X2O2L3X3O3A3F2M0F3'
 ROOM = 768
 LEFT = 32
 ANY = pl.ANY
 MESH = pl.DeviceIdType.MESH
 
 
-def load_table(table, wide, stage, sems, first=0):
+def load_table(table, wide, stage, sems):
     rows = table.shape[0]
     n_chunks = rows // CHUNK
 
@@ -39,17 +42,17 @@
         copy(k).wait()
         buf = stage.at[k % 2]
 
-        @pl.loop(0, CHUNK // 32)
+        @pl.loop(0, CHUNK // (TILE * SUB))
         def _(g):
-            for i in range(4):
-                r8 = pl.multiple_of((g * 4 + i) * 8, 8)
-                w8 = pl.multiple_of((first + k * CHUNK + (g * 4 + i) * 8) * SUB, 32)
+            for i in range(SUB):
+                r8 = pl.multiple_of((g * SUB + i) * TILE, TILE)
+                w8 = pl.multiple_of((k * CHUNK + (g * SUB + i) * TILE) * SUB, (TILE * SUB))
                 for j in range(SUB):
                     if j < SUB - 1:
-                        wide[pl.ds(w8 + j, 8, stride=SUB), :] = buf[pl.ds(r8, 8), j * LANES:(j + 1) * LANES]
+                        wide[pl.ds(w8 + j, TILE, stride=SUB), :] = buf[pl.ds(r8, TILE), j * LANES:(j + 1) * LANES]
                     else:
-                        wide[pl.ds(w8 + j, 8, stride=SUB), :] = jnp.concatenate(
-                            [buf[pl.ds(r8, 8), j * LANES:j * LANES + TAIL], jnp.zeros((8, LANES - TAIL), jnp.float32)],
+                        wide[pl.ds(w8 + j, TILE, stride=SUB), :] = jnp.concatenate(
+                            [buf[pl.ds(r8, TILE), j * LANES:j * LANES + TAIL], jnp.zeros((TILE, LANES - TAIL), jnp.float32)],
                             axis=1)
 
 
@@ -65,17 +68,17 @@
             copy(k - 2).wait()
         buf = stage.at[k % 2]
 
-        @pl.loop(0, CHUNK // 32)
+        @pl.loop(0, CHUNK // (TILE * SUB))
         def _(g):
-            for i in range(4):
-                r8 = pl.multiple_of((g * 4 + i) * 8, 8)
-                w8 = pl.multiple_of((k * CHUNK + (g * 4 + i) * 8) * SUB, 32)
+            for i in range(SUB):
+                r8 = pl.multiple_of((g * SUB + i) * TILE, TILE)
+                w8 = pl.multiple_of((k * CHUNK + (g * SUB + i) * TILE) * SUB, (TILE * SUB))
                 for j in range(SUB):
                     piece = value(w8, j)
                     if j < SUB - 1:
-                        buf[pl.ds(r8, 8), j * LANES:(j + 1) * LANES] = piece
+                        buf[pl.ds(r8, TILE), j * LANES:(j + 1) * LANES] = piece
                     else:
-                        buf[pl.ds(r8, 8), j * LANES:j * LANES + TAIL] = piece[:, :TAIL]
+                        buf[pl.ds(r8, TILE), j * LANES:j * LANES + TAIL] = piece[:, :TAIL]
 
         copy(k).start()
     copy(n_chunks - 2).wait()
@@ -85,10 +88,10 @@
 def pick_kernel(rows4, table, out, wide, stage, sems):
     load_table(table, wide, stage, sems)
 
-    @pl.loop(0, SLOTS // 16)
+    @pl.loop(0, SLOTS // UNROLL)
     def _(g):
-        for i in range(16):
-            k = g * 16 + i
+        for i in range(UNROLL):
+            k = g * UNROLL + i
             r4 = pl.multiple_of(rows4[k], SUB)
             out[pl.ds(pl.multiple_of(k * SUB, SUB), SUB), :] = wide[pl.ds(r4, SUB), :]
 
@@ -110,10 +113,10 @@
 def add_kernel(rows4, table, grads, out, wide, stage, sems):
     load_table(table, wide, stage, sems)
 
-    @pl.loop(0, SLOTS // 16)
+    @pl.loop(0, SLOTS // UNROLL)
     def _(g):
-        for i in range(16):
-            k = g * 16 + i
+        for i in range(UNROLL):
+            k = g * UNROLL + i
             r4 = pl.multiple_of(rows4[k], SUB)
             wide[pl.ds(r4, SUB), :] = wide[pl.ds(r4, SUB), :] - LEARN_RATE * grads[pl.ds(pl.multiple_of(k * SUB, SUB), SUB), :]
 
@@ -135,20 +138,21 @@
         name='add_rows')(rows4, table, grads)
 
 
-def score_kernel(bounds, row4s, slot4s, own, other, u_blk, own_grad, other_grad, gu_blk, loss_blk,
-                 wide, grad, stage, sems, prods, coef):
+def score_kernel(bounds, row4s, slot4s, tables, u_blk, own_grad, other_grad, gu_blk, loss_blk,
+                 wide, grad, sems, prods, coef):
     step = pl.program_id(0)
-    rows = own.shape[0]
 
     @pl.when(step == 0)
     def _():
-        load_table(own, wide, stage, sems)
-        load_table(other, wide, stage, sems, rows)
+        whole = pltpu.make_async_copy(tables, wide, sems.at[0])
+        whole.start()
         loss_blk[...] = jnp.zeros_like(loss_blk)
 
-        @pl.loop(0, grad.shape[0] // 256)
+        @pl.loop(0, grad.shape[0] // COLS)
         def _(g):
-            grad[pl.ds(pl.multiple_of(g * 256, 256), 256), :] = jnp.zeros((256, LANES), jnp.float32)
+            grad[pl.ds(pl.multiple_of(g * COLS, COLS), COLS), :] = jnp.zeros((COLS, LANES), jnp.float32)
+
+        whole.wait()
 
     @pl.loop(0, SLOTS * SUB // 128)
     def _(g):
@@ -205,59 +209,33 @@
 
     @pl.when(step == pl.num_programs(0) - 1)
     def _():
-        first = pltpu.make_async_copy(grad.at[pl.ds(0, rows * SUB)], own_grad, sems.at[0])
-        second = pltpu.make_async_copy(grad.at[pl.ds(rows * SUB, rows * SUB)], other_grad, sems.at[1])
+        half = own_grad.shape[0]
+        first = pltpu.make_async_copy(grad.at[pl.ds(0, half)], own_grad, sems.at[0])
+        second = pltpu.make_async_copy(grad.at[pl.ds(half, half)], other_grad, sems.at[1])
         first.start()
         second.start()
         first.wait()
         second.wait()
 
 
-def score_rows(bounds, row4s, slot4s, own, other, u_all):
-    rows, width = own.shape
+def score_rows(bounds, row4s, slot4s, tables, u_all):
     n_blocks = u_all.shape[0] // (SLOTS * SUB)
     blk = pl.BlockSpec((SLOTS * SUB, LANES), lambda i, *_: (i, 0))
-    half = jax.ShapeDtypeStruct((rows * SUB, LANES), jnp.float32)
+    half = jax.ShapeDtypeStruct((tables.shape[0] // 2, LANES), jnp.float32)
     return pl.pallas_call(
         score_kernel,
         out_shape=(half, half, jax.ShapeDtypeStruct(u_all.shape, jnp.float32),
                    jax.ShapeDtypeStruct((8, LANES), jnp.float32)),
         grid_spec=pltpu.PrefetchScalarGridSpec(
             num_scalar_prefetch=3, grid=(n_blocks,),
-            in_specs=[pl.BlockSpec(memory_space=ANY), pl.BlockSpec(memory_space=ANY), blk],
+            in_specs=[pl.BlockSpec(memory_space=ANY), blk],
             out_specs=(pl.BlockSpec(memory_space=ANY), pl.BlockSpec(memory_space=ANY), blk,
                        pl.BlockSpec((8, LANES), lambda i, *_: (0, 0))),
-            scratch_shapes=[pltpu.VMEM((2 * rows * SUB, LANES), jnp.float32),
-                            pltpu.VMEM((2 * rows * SUB, LANES), jnp.float32),
-                            pltpu.VMEM((2, CHUNK, width), jnp.float32),
-                            pltpu.SemaphoreType.DMA((2,)),
+            scratch_shapes=[*[pltpu.VMEM(tables.shape, jnp.float32)] * 2, pltpu.SemaphoreType.DMA((2,)),
                             pltpu.VMEM((BATCH * SUB, LANES), jnp.float32),
                             pltpu.VMEM((BATCH * SUB, LANES), jnp.float32)]),
         compiler_params=pltpu.CompilerParams(vmem_limit_bytes=60 * 1024 * 1024),
-        name='score_rows')(bounds, row4s, slot4s, own, other, u_all)
-
-
-def finish_kernel(table, first, second, out):
-    @pl.loop(0, CHUNK // 32)
-    def _(g):
-        for i in range(4):
-            r8 = pl.multiple_of((g * 4 + i) * 8, 8)
-            w8 = pl.multiple_of((g * 4 + i) * 8 * SUB, 32)
-            for j in range(SUB):
-                cols = slice(j * LANES, (j + 1) * LANES if j < SUB - 1 else j * LANES + TAIL)
-                grad = first[pl.ds(w8 + j, 8, stride=SUB), :] + second[pl.ds(w8 + j, 8, stride=SUB), :]
-                if j == SUB - 1:
-                    grad = grad[:, :TAIL]
-                out[pl.ds(r8, 8), cols] = table[pl.ds(r8, 8), cols] - LEARN_RATE * grad
-
-
-def finish_rows(table, first, second):
-    rows, width = table.shape
-    native = pl.BlockSpec((CHUNK, width), lambda i: (i, 0))
-    wide = pl.BlockSpec((CHUNK * SUB, LANES), lambda i: (i, 0))
-    return pl.pallas_call(
-        finish_kernel, out_shape=jax.ShapeDtypeStruct(table.shape, jnp.float32), grid=(rows // CHUNK,),
-        in_specs=[native, wide, wide], out_specs=native, name='finish_rows')(table, first, second)
+        name='score_rows')(bounds, row4s, slot4s, tables, u_all)
 
 
 def place_of():
@@ -286,8 +264,11 @@
     return z, near, 6 - far - near - z, far
 
 
-def meet_neighbours(me, x_peer, y_peer, below, above):
+def meet_neighbours(me, x_peer, y_peer, below, above, partner=None):
     barrier = pltpu.get_barrier_semaphore()
+    extra = int(partner is not None)
+    if extra:
+        pl.semaphore_signal(barrier, inc=1, device_id=(partner,), device_id_type=MESH)
     pl.semaphore_signal(barrier, inc=1, device_id=(x_peer,), device_id_type=MESH)
     pl.semaphore_signal(barrier, inc=1, device_id=(y_peer,), device_id_type=MESH)
 
@@ -301,11 +282,11 @@
 
     @pl.when(below & above)
     def _():
-        pl.semaphore_wait(barrier, 4)
+        pl.semaphore_wait(barrier, 4 + extra)
 
     @pl.when(~(below & above))
     def _():
-        pl.semaphore_wait(barrier, 3)
+        pl.semaphore_wait(barrier, 3 + extra)
 
 
 def remote(src, dst, send, recv, peer):
@@ -318,7 +299,8 @@
     return rows // 2 - small, small
 
 
-def gather_kernel(mine, out, zs, zr, xs, xr, ys, yr, gs, gr, local_sem):
+def gather_kernel(mine, own_t, other_t, out, tables, cols, rows, in_sem, out_sem,
+                  zs, zr, xs, xr, ys, yr, gs, gr, local_sem):
     me, x, y, z, far_x, far_y, x_peer, y_peer, below, above = place_of()
     big, small = shares(mine.shape[0])
     low, high, both = pl.ds(0, big), pl.ds(big, big), pl.ds(0, 2 * big)
@@ -457,7 +439,44 @@
             def _():
                 late_down(p).start()
 
-    follow(GATHER_PLAN, {'I': late_out, 'J': late_on, 'Z': along_z, 'P': early_pieces, 'Q': other_pieces,
+    def convert(k):
+        source, first = (own_t, k) if k < TURNS else (other_t, k - TURNS)
+
+        def fetch(t):
+            at = pl.ds(pl.multiple_of((first * TURNS + t) * COLS, COLS), COLS)
+            return pltpu.make_async_copy(source.at[:, at], cols.at[t % 2], in_sem.at[t % 2])
+
+        def put(t):
+            at = pl.ds(pl.multiple_of((k * TURNS + t) * COLS * SUB, COLS), COLS * SUB)
+            return pltpu.make_async_copy(rows.at[t % 2], tables.at[at], out_sem.at[t % 2])
+
+        fetch(0).start()
+
+        @pl.loop(0, TURNS)
+        def _(t):
+            fetch(t).wait()
+
+            @pl.when(t + 1 < TURNS)
+            def _():
+                fetch(t + 1).start()
+
+            @pl.when(t > 1)
+            def _():
+                put(t - 2).wait()
+
+            for h in range(COLS // LANES):
+                for j in range(SUB):
+                    width = LANES if j < SUB - 1 else TAIL
+                    turned = cols[t % 2, j * LANES:j * LANES + width, h * LANES:(h + 1) * LANES].T
+                    if width < LANES:
+                        turned = jnp.concatenate([turned, jnp.zeros((LANES, LANES - width), jnp.float32)], axis=1)
+                    rows[t % 2, pl.ds(h * LANES * SUB + j, LANES, stride=SUB), :] = turned
+            put(t).start()
+
+        put(TURNS - 2).wait()
+        put(TURNS - 1).wait()
+
+    follow(GATHER_PLAN, {'X': convert, 'I': late_out, 'J': late_on, 'Z': along_z, 'P': early_pieces, 'Q': other_pieces,
                          'R': relay, 'G': late_along_z})
     for piece in (late1_x(), late1_y(), late2_x(), late2_y()):
         piece.wait_send()
@@ -483,22 +502,25 @@
             late_down(p).wait_send()
 
 
-def gather_slots(mine):
+def gather_slots(mine, own_t, other_t):
     rows = mine.shape[0]
+    width, words = own_t.shape
     dma = pltpu.SemaphoreType.DMA
-    out = pl.pallas_call(
+    out, tables = pl.pallas_call(
         gather_kernel,
-        out_shape=jax.ShapeDtypeStruct((4, 2, 2, rows, LANES), jnp.float32),
-        in_specs=[pl.BlockSpec(memory_space=pltpu.VMEM)],
-        out_specs=pl.BlockSpec(memory_space=ANY),
-        scratch_shapes=[dma((4, 4)), dma((4, 4)), *[dma((3, 4))] * 4,
+        out_shape=(jax.ShapeDtypeStruct((4, 2, 2, rows, LANES), jnp.float32),
+                   jax.ShapeDtypeStruct((2 * words * SUB, LANES), jnp.float32)),
+        in_specs=[pl.BlockSpec(memory_space=pltpu.VMEM), *[pl.BlockSpec(memory_space=ANY)] * 2],
+        out_specs=(pl.BlockSpec(memory_space=ANY),) * 2,
+        scratch_shapes=[pltpu.VMEM((2, width, COLS), jnp.float32), pltpu.VMEM((2, COLS * SUB, LANES), jnp.float32),
+                        dma((2,)), dma((2,)), dma((4, 4)), dma((4, 4)), *[dma((3, 4))] * 4,
                         dma((4,)), dma((4,)), dma],
         compiler_params=pltpu.CompilerParams(collective_id=1, has_side_effects=True),
-        name='gather_slots')(mine)
-    return out.reshape(16 * rows, LANES)
-
-
-def scatter_kernel(parts, out, r1x, r1y, r2x, r2y, zu, zd, stage, lu, ld, held, ly2, lx1, lx2, ly1,
+        name='gather_slots')(mine, own_t, other_t)
+    return out.reshape(16 * rows, LANES), tables
+
+
+def scatter_kernel(parts, tables, own_grad, other_grad, out, new_table, back, terms, fresh, term_sem, fresh_sem, swap_s, swap_r, r1x, r1y, r2x, r2y, zu, zd, stage, lu, ld, held, ly2, lx1, lx2, ly1,
                    zs, zr, xs, xr, ys, yr, gs, gr, stage_sem, held_sem):
     me, x, y, z, far_x, far_y, x_peer, y_peer, below, above = place_of()
     half, small = shares(out.shape[0])
@@ -616,7 +638,10 @@
     def late_y2():
         return remote(lx1.at[far_y], ly2, *pair(gs, gr, 3), y_peer)
 
-    meet_neighbours(me, x_peer, y_peer, below, above)
+    partner = me + 1 - 2 * (me % 2)
+    meet_neighbours(me, x_peer, y_peer, below, above, partner)
+    swap = remote(other_grad, back, swap_s, swap_r, partner)
+    swap.start()
     for i in range(4):
         load(0, i).start()
 
@@ -701,7 +726,51 @@
         late_x2().start()
         late_y2().start()
 
-    follow(SCATTER_PLAN, {'E': late_ends, 'N': first_pieces, 'O': other_pieces, 'A': turn_corner, 'F': finish,
+    def update(k):
+        if k == 0:
+            swap.wait_recv()
+
+        def fetch(t):
+            at = pl.ds(pl.multiple_of((k * TURNS + t) * COLS * SUB, COLS), COLS * SUB)
+            return [pltpu.make_async_copy(ref.at[at], terms.at[i, t % 2], term_sem.at[i, t % 2])
+                    for i, ref in enumerate((tables, own_grad, back))]
+
+        def put(t):
+            at = pl.ds(pl.multiple_of((k * TURNS + t) * COLS, COLS), COLS)
+            return pltpu.make_async_copy(fresh.at[t % 2], new_table.at[at], fresh_sem.at[t % 2])
+
+        for copy in fetch(0):
+            copy.start()
+
+        @pl.loop(0, TURNS)
+        def _(t):
+            for copy in fetch(t):
+                copy.wait()
+
+            @pl.when(t + 1 < TURNS)
+            def _():
+                for copy in fetch(t + 1):
+                    copy.start()
+
+            @pl.when(t > 1)
+            def _():
+                put(t - 2).wait()
+
+            @pl.loop(0, COLS // TILE)
+            def _(g):
+                for j in range(SUB):
+                    at = pl.ds(pl.multiple_of(g * TILE * SUB, TILE) + j, TILE, stride=SUB)
+                    old, first, second = [terms[i, t % 2, at, :] for i in range(3)]
+                    new = old - LEARN_RATE * (first + second)
+                    width = LANES if j < SUB - 1 else TAIL
+                    fresh[t % 2, pl.ds(pl.multiple_of(g * TILE, TILE), TILE), j * LANES:j * LANES + width] = new[:, :width]
+
+            put(t).start()
+
+        put(TURNS - 2).wait()
+        put(TURNS - 1).wait()
+
+    follow(SCATTER_PLAN, {'X': update, 'E': late_ends, 'N': first_pieces, 'O': other_pieces, 'A': turn_corner, 'F': finish,
                           'L': late_stage, 'M': late_corner})
 
     @pl.loop(0, half // STEP)
@@ -719,7 +788,7 @@
         out[block_of(g, 2 * half), :] = ly1[x, rows, :] + lx2[rows, :]
         out[block_of(g, 2 * half + small), :] = lx1[y, rows, :] + ly2[rows, :]
 
-    for piece in (late_x1(), late_y1(), late_x2(), late_y2()):
+    for piece in (late_x1(), late_y1(), late_x2(), late_y2(), swap):
         piece.wait_send()
 
     for k in range(4):
@@ -749,17 +818,20 @@
                     down(c, k, total).wait_send()
 
 
-def scatter_slots(parts):
+def scatter_slots(parts, tables, own_grad, other_grad, width):
     rows = parts.shape[0] // 16
     dma = pltpu.SemaphoreType.DMA
     half, small = shares(rows)
     f32 = jnp.float32
     return pl.pallas_call(
         scatter_kernel,
-        out_shape=jax.ShapeDtypeStruct((rows, LANES), f32),
-        in_specs=[pl.BlockSpec(memory_space=ANY)],
-        out_specs=pl.BlockSpec(memory_space=pltpu.VMEM),
-        scratch_shapes=[*[pltpu.VMEM((4, 2, half, LANES), f32)] * 2, *[pltpu.VMEM((4, half, LANES), f32)] * 2,
+        out_shape=(jax.ShapeDtypeStruct((rows, LANES), f32),
+                   jax.ShapeDtypeStruct((own_grad.shape[0] // SUB, width), f32),
+                   jax.ShapeDtypeStruct(own_grad.shape, f32)),
+        in_specs=[pl.BlockSpec(memory_space=ANY)] * 4,
+        out_specs=(pl.BlockSpec(memory_space=pltpu.VMEM), *[pl.BlockSpec(memory_space=ANY)] * 2),
+        scratch_shapes=[pltpu.VMEM((3, 2, COLS * SUB, LANES), f32), pltpu.VMEM((2, COLS, width), f32),
+                        dma((3, 2)), dma((2,)), dma, dma, *[pltpu.VMEM((4, 2, half, LANES), f32)] * 2, *[pltpu.VMEM((4, half, LANES), f32)] * 2,
                         *[pltpu.VMEM((2, 3, half, LANES), f32)] * 2, pltpu.VMEM((4, half, LANES), f32),
                         *[pltpu.VMEM((3, 2, 2, 2 * small, LANES), f32)] * 2,
                         pltpu.VMEM((2, 2, 2 * small, LANES), f32),
@@ -768,7 +840,11 @@
                         *[dma((4,))] * 3, dma],
         compiler_params=pltpu.CompilerParams(collective_id=2, has_side_effects=True,
                                              vmem_limit_bytes=63 * 1024 * 1024),
-        name='scatter_slots')(parts.reshape(4, 2, 2, rows, LANES))
+        name='scatter_slots')(parts.reshape(4, 2, 2, rows, LANES), tables, own_grad, other_grad)[:2]
+
+
+def trade(a):
+    return lax.all_to_all(a, 'ep', 0, 0)
 
 
 def solution(mesh):
@@ -783,7 +859,7 @@
         partner = [(d, d + 1 - 2 * (d % 2)) for d in range(group)]
         other_out = lax.ppermute(table_out, 'ep', partner)
 
-        all_centers = lax.all_to_all(jnp.broadcast_to(centers[None], (group, n_pairs)), 'ep', 0, 0).reshape(-1)
+        all_centers = trade(jnp.broadcast_to(centers[None], (group, n_pairs))).reshape(-1)
         all_owner = all_centers % group
         counts = jnp.sum((all_owner.reshape(group, n_pairs)[:, None, :] == ids[None, :, None]).astype(jnp.int32), axis=2)
         totals = jnp.sum(counts, axis=0)
@@ -817,7 +893,7 @@
         keys = jnp.concatenate([dest.reshape(n_ref), spare_dest.reshape(group * ROOM)])
         vals = jnp.concatenate([code.reshape(n_ref), jnp.full((group * ROOM,), big)])
         _, vals = lax.sort((keys, vals), num_keys=1, is_stable=False)
-        got = lax.all_to_all(vals[:group * ROOM].reshape(group, ROOM), 'ep', 0, 0)
+        got = trade(vals[:group * ROOM].reshape(group, ROOM))
         refs = lax.sort(got.reshape(group * ROOM), is_stable=False)
         edges = jnp.arange(group + 1, dtype=jnp.int32) * (SLOTS * rows_dev * 2)
         bounds = jnp.sum((refs[None, :] < edges[:, None]).astype(jnp.int32), axis=1)
@@ -825,16 +901,14 @@
         row4s = jnp.concatenate([refs % (2 * rows_dev) * SUB, pad])
         slot4s = jnp.concatenate([refs // (2 * rows_dev) % SLOTS * SUB, pad])
 
-        u_all = gather_slots(u_mine)
-        own_grad, other_grad, gu, loss = score_rows(bounds, row4s, slot4s, table_out, other_out, u_all)
-        back_grad = lax.ppermute(other_grad, 'ep', partner)
-        gu_mine = scatter_slots(gu)
+        u_all, tables = gather_slots(u_mine, table_out.T, other_out.T)
+        own_grad, other_grad, gu, loss = score_rows(bounds, row4s, slot4s, tables, u_all)
+        gu_mine, new_out = scatter_slots(gu, tables, own_grad, other_grad, width)
         new_in = add_rows(rows4, table_in, gu_mine)
-        new_out = finish_rows(table_out, own_grad, back_grad)
         loss = jnp.sum(loss[:, 0])
         overflow = jnp.sum((~fits).astype(jnp.int32))
         both = jnp.where(jnp.arange(LANES) == 0, loss, overflow.astype(jnp.float32))
-        sums = jnp.sum(lax.all_to_all(jnp.broadcast_to(both[None], (group, LANES)), 'ep', 0, 0), axis=0)
+        sums = jnp.sum(trade(jnp.broadcast_to(both[None], (group, LANES))), axis=0)
 
         def more(state):
             return state[0] < jnp.where(sums[1] > 0.5, n_pairs // LEFT, 0)
@@ -849,7 +923,9 @@
             left = cut((~fits).astype(jnp.int32))[:, None] == 1
             held = word % group == me
             row = word // group
-            found = jnp.concatenate([table_in[row[:, :1]], table_out[row[:, 1:]]], axis=1)
+            parts = row[:, 1:, None] * SUB + jnp.arange(SUB)
+            o_rows = tables[parts].reshape(row.shape[0], n_neg + 1, SUB * LANES)[:, :, :width]
+            found = jnp.concatenate([table_in[row[:, :1]], o_rows], axis=1)
             found = lax.psum(jnp.where(held[:, :, None], found, 0.0), 'ep')
             u_vec, o_vec = found[:, 0], found[:, 1:]
             sign = jnp.where(is_ctx == 1, -1.0, 1.0)

time: 911 us -> 889 us (0.976)
  local copies, waits for them, and re-layouts: 51.6 us -> 34.1 us
  Pallas kernels: 763 us -> 747 us
  starting transfers between devices: 24.6 us -> 34.5 us
    pallas_call x3 -> x2, Pallas kernels: 583 us -> 569 us  [the longest x1 285 us: scatter_slots(): pl.pallas_call(scatter_kernel, out_shape=(jax.ShapeDtypeStruct((rows, LAN...]
    all_to_all x3, starting transfers between devices: 23.9 us -> 33.9 us  [trade(): return lax.all_to_all(a, 'ep', 0, 0)]
    unnamed x7 -> x6, local copies, waits for them, and re-layouts: 35.7 us -> 27.3 us
  transfers between devices with their start and end apart: 5 -> 4, of which waited for: 0 -> 0; matrix products, arithmetic and copies ran while one was open for 8% -> 6% of each run, Pallas kernels for 66% -> 36%
where the time goes in v5:
time: 889 us; the launch traced here: 878 us
  Pallas kernels  747 us (84%)
  other arithmetic  43.7 us (5%)
  starting transfers between devices  34.5 us (4%)
  local copies, waits for them, and re-layouts  34.1 us (4%)
  between operations  17.1 us (2%)
    pallas_call x1, Pallas kernels, scatter_slots(): pl.pallas_call(scatter_kernel, out_shape=(jax.ShapeDtypeStruct((rows, LAN...  285 us
    pallas_call x1, Pallas kernels, gather_slots(): pl.pallas_call(gather_kernel, out_shape=(jax.ShapeDtypeStruct((4, 2, 2, r...  284 us
    pallas_call x1, Pallas kernels, score_rows(): pl.pallas_call(score_kernel, out_shape=(half, half, jax.ShapeDtypeStruct(...  150 us
    all_to_all x3, starting transfers between devices, trade(): return lax.all_to_all(a, 'ep', 0, 0)  33.9 us
    unnamed x6, local copies, waits for them, and re-layouts  27.3 us
    sort x1, other arithmetic, device_step(): _, vals = lax.sort((keys, vals), num_keys=1, is_stable=False)  19.2 us
    pallas_call x1, Pallas kernels, add_rows(): pl.pallas_call(add_kernel, out_shape=jax.ShapeDtypeStruct(table.shape, jn...  18.2 us
  transfers between devices with their start and end apart: 4, of which 0 were waited for; matrix products, arithmetic and copies ran while one was open for 6% of the time, Pallas kernels for 36%

profile of v5, /device:TPU:0, one launch (start us, length us, event | category | flops | bytes accessed | tf_op | source)
XLA Modules:
  0.0 877.7 jit_solution(10296105816435530906)
XLA Ops:
  7.7 1.4 broadcast_in_dim.176
  9.2 7.0 all-to-all-start
  16.1 0.9 pad_add_fusion.2
  17.0 0.7 fusion.40
  18.5 9.1 %copy.111.table = f32[4096,500]{1,0:T(8,128)} copy(f32[4096,500]{0,1:T(8,128)} %param.7) | data formatting | bytes 16384000 | tf_op args[0]
  27.8 7.3 sort.29
  40.9 19.2 %sort.30 = (s32[40960]{0:T(1024)}, s32[40960]{0:T(1024)S(1)}) sort(s32[40960]{0:T(1024)S(1)} %pad_add_fusion.1, s32[40960]{0:T(1024)S(1)} %concatenate.39), dimensions={0}, to_apply=%region_6.7 | sort | flops 655360 | bytes 655360 | tf_op jit(solution)/shard_map/sort | solution.py:895
  60.1 0.6 slice.60
  60.7 24.4 %all-to-all-start.1 = ((s32[32,1,768]{2,1,0:T(1,128)}), s32[32,1,768]{2,1,0:T(1,128)S(1)}, u32[]{:S(2)}, u32[]{:S(2)}) async-start(s32[32,1,768]{2,1,0:T(1,128)} %bitcast.2), calls=%async_computation.1 | async-start | bytes 196608 | tf_op jit(solution)/shard_map/all_to_all | solution.py:847
  85.7 9.8 %pick_rows.1.mine = f32[4992,128]{1,0:T(8,128)} custom-call(s32[1248]{0:T(1024)} %fusion.38.rows4, f32[4096,500]{1,0:T(8,128)} %copy.111.table), custom_call_target="tpu_custom_call" | custom-call | tf_op jit(solution)/shard_map/pick_rows/pallas_call | solution.py:100
  95.5 8.6 sort.31
  104.9 0.6 concatenate.40.row4s
  105.6 1.2 convert_reduce_fusion.1.bounds
  106.8 284.4 %gather_slots.1 = (f32[4,2,2,4992,128]{4,3,2,1,0:T(8,128)}, f32[32768,128]{1,0:T(8,128)}) custom-call(f32[4992,128]{1,0:T(8,128)} %pick_rows.1.mine, f32[500,4096]{1,0:T(8,128)} %bitcast.64, f32[500,4096]{1,0:T(8,128)} %bitcast.5.other_t), custom_call_target="tpu_custom_call" | custom-call | tf_op jit(solution)/shard_map/gather_slots/pallas_call | solution.py:509
  391.2 149.7 %score_rows.1 = (f32[16384,128]{1,0:T(8,128)}, f32[16384,128]{1,0:T(8,128)}, f32[79872,128]{1,0:T(8,128)}, f32[8,128]{1,0:T(8,128)}) custom-call(s32[33]{0:T(128)} %convert_reduce_fusion.1.bounds, s32[24640]{0:T(1024)} %concatenate.40.row4s, s32[24640]{0:T(1024)} %concatenate.41.slot4s, f32[32768,128]{1,0:T(8,128)} %get-tuple-element.522.tables, ...), custom_call_target="tpu_custom_call" | custom-call | tf_op jit(solution)/shard_map/score_rows/pallas_call | solution.py:225
  540.9 1.3 slice_reduce_fusion
  542.2 0.6 compare_select_fusion.8
  543.5 2.5 all-to-all-start.2
  546.0 285.0 %scatter_slots.1 = (f32[4992,128]{1,0:T(8,128)}, f32[4096,500]{1,0:T(8,128)}, f32[16384,128]{1,0:T(8,128)}) custom-call(f32[4,2,2,4992,128]{4,3,2,1,0:T(8,128)} %bitcast.62, f32[32768,128]{1,0:T(8,128)} %get-tuple-element.522.tables, f32[16384,128]{1,0:T(8,128)} %get-tuple-element.190.own_grad, f32[16384,128]{1,0:T(8,128)} %get-tuple-element.191.other_grad), custom_call_target="tpu_custom_call" | custom-call | tf_op jit(solution)/shard_map/scatter_slots/pallas_call | solution.py:826
  831.0 18.2 %add_rows.1 = f32[4096,500]{1,0:T(8,128)} custom-call(s32[1248]{0:T(1024)} %fusion.38.rows4, f32[4096,500]{1,0:T(8,128)} %copy.111.table, f32[4992,128]{1,0:T(8,128)} %get-tuple-element.192.grads), custom_call_target="tpu_custom_call" | custom-call | tf_op jit(solution)/shard_map/add_rows/pallas_call | solution.py:127
  849.8 1.8 while.18
  849.8 1.2 slice.101
  851.6 8.9 %copy.114 = f32[4096,500]{0,1:T(8,128)} copy(f32[4096,500]{1,0:T(8,128)} %get-tuple-element.376) | data formatting | bytes 16384000
  860.5 8.9 %copy.115 = f32[4096,500]{0,1:T(8,128)} copy(f32[4096,500]{1,0:T(8,128)} %get-tuple-element.377) | data formatting | bytes 16384000
  (41 shorter events, 8.5 us)
Async XLA Ops:
  7.2 99.6 %collective-permute-start = (f32[4096,500]{0,1:T(8,128)}, f32[4096,500]{0,1:T(8,128)}, u32[]{:S(2)}, u32[]{:S(2)}) collective-permute-start(f32[4096,500]{0,1:T(8,128)} %param.8), channel_id=1, source_target_pairs={{0,1},{1,0},{2,3},{3,2},{4,5},{5,4},{6,7},{7,6},{8,9},{9,8},{10,11... | collective-permute-start | bytes 24576008 | tf_op jit(solution)/shard_map/ppermute | solution.py:860
  9.2 18.5 %all-to-all-start = ((s32[32,1,1024]{2,1,0:T(1,128)}), s32[32,1,1024]{2,1,0:T(1,128)S(1)}, u32[]{:S(2)}, u32[]{:S(2)}) async-start(s32[32,1,1024]{2,1,0:T(1,128)} %broadcast_in_dim.176), calls=%async_computation | async-start | bytes 262144 | tf_op jit(solution)/shard_map/all_to_all | solution.py:847
  60.7 34.8 %all-to-all-start.1 = ((s32[32,1,768]{2,1,0:T(1,128)}), s32[32,1,768]{2,1,0:T(1,128)S(1)}, u32[]{:S(2)}, u32[]{:S(2)}) async-start(s32[32,1,768]{2,1,0:T(1,128)} %bitcast.2), calls=%async_computation.1 | async-start | bytes 196608 | tf_op jit(solution)/shard_map/all_to_all | solution.py:847
  543.5 305.8 %all-to-all-start.2 = ((f32[32,1,128]{2,1,0:T(1,128)}), f32[32,1,128]{2,1,0:T(1,128)S(1)}, u32[]{:S(2)}, u32[]{:S(2)}) async-start(f32[32,1,128]{2,1,0:T(1,128)} %broadcast_in_dim.189), calls=%async_computation.2 | async-start | bytes 32768 | tf_op jit(solution)/shard_map/all_to_all | solution.py:847
  849.3 0.5 copy-start.10

commit v6 on v5

--- a/solution.py
+++ b/solution.py
@@ -258,6 +258,10 @@
     return sends.at[at], recvs.at[at]
 
 
+def partner_of(me):
+    return me + 1 - 2 * (me % 2)
+
+
 def plane_order(z):
     far = 3 * (1 - z // 2)
     near = 1 + z % 2
@@ -299,7 +303,7 @@
     return rows // 2 - small, small
 
 
-def gather_kernel(mine, own_t, other_t, out, tables, cols, rows, in_sem, out_sem,
+def gather_kernel(mine, own_t, out, tables, other_t, cols, rows, in_sem, out_sem, swap_s, swap_r,
                   zs, zr, xs, xr, ys, yr, gs, gr, local_sem):
     me, x, y, z, far_x, far_y, x_peer, y_peer, below, above = place_of()
     big, small = shares(mine.shape[0])
@@ -364,13 +368,16 @@
         piece = out.at[z, :, x, late_y]
         return remote(piece, piece, *pair(gs, gr, 3), x_peer)
 
-    meet_neighbours(me, x_peer, y_peer, below, above)
+    partner = partner_of(me)
+    meet_neighbours(me, x_peer, y_peer, below, above, partner)
+    swap = remote(own_t, other_t, swap_s, swap_r, partner)
     keep = pltpu.make_async_copy(mine, out.at[z, y, x], local_sem)
     keep.start()
 
     def late_out(k):
         late1_x().start()
         late1_y().start()
+        swap.start()
 
     def late_on(k):
         keep.wait()
@@ -441,6 +448,8 @@
 
     def convert(k):
         source, first = (own_t, k) if k < TURNS else (other_t, k - TURNS)
+        if k == TURNS:
+            swap.wait_recv()
 
         def fetch(t):
             at = pl.ds(pl.multiple_of((first * TURNS + t) * COLS, COLS), COLS)
@@ -478,7 +487,7 @@
 
     follow(GATHER_PLAN, {'X': convert, 'I': late_out, 'J': late_on, 'Z': along_z, 'P': early_pieces, 'Q': other_pieces,
                          'R': relay, 'G': late_along_z})
-    for piece in (late1_x(), late1_y(), late2_x(), late2_y()):
+    for piece in (late1_x(), late1_y(), late2_x(), late2_y(), swap):
         piece.wait_send()
     for k in range(4):
         from_y(k, 1, x, high).wait_recv()
@@ -502,21 +511,22 @@
             late_down(p).wait_send()
 
 
-def gather_slots(mine, own_t, other_t):
+def gather_slots(mine, own_t):
     rows = mine.shape[0]
     width, words = own_t.shape
     dma = pltpu.SemaphoreType.DMA
-    out, tables = pl.pallas_call(
+    out, tables, _ = pl.pallas_call(
         gather_kernel,
         out_shape=(jax.ShapeDtypeStruct((4, 2, 2, rows, LANES), jnp.float32),
-                   jax.ShapeDtypeStruct((2 * words * SUB, LANES), jnp.float32)),
-        in_specs=[pl.BlockSpec(memory_space=pltpu.VMEM), *[pl.BlockSpec(memory_space=ANY)] * 2],
-        out_specs=(pl.BlockSpec(memory_space=ANY),) * 2,
+                   jax.ShapeDtypeStruct((2 * words * SUB, LANES), jnp.float32),
+                   jax.ShapeDtypeStruct(own_t.shape, jnp.float32)),
+        in_specs=[pl.BlockSpec(memory_space=pltpu.VMEM), pl.BlockSpec(memory_space=ANY)],
+        out_specs=(pl.BlockSpec(memory_space=ANY),) * 3,
         scratch_shapes=[pltpu.VMEM((2, width, COLS), jnp.float32), pltpu.VMEM((2, COLS * SUB, LANES), jnp.float32),
-                        dma((2,)), dma((2,)), dma((4, 4)), dma((4, 4)), *[dma((3, 4))] * 4,
+                        dma((2,)), dma((2,)), dma, dma, dma((4, 4)), dma((4, 4)), *[dma((3, 4))] * 4,
                         dma((4,)), dma((4,)), dma],
         compiler_params=pltpu.CompilerParams(collective_id=1, has_side_effects=True),
-        name='gather_slots')(mine, own_t, other_t)
+        name='gather_slots')(mine, own_t)
     return out.reshape(16 * rows, LANES), tables
 
 
@@ -638,7 +648,7 @@
     def late_y2():
         return remote(lx1.at[far_y], ly2, *pair(gs, gr, 3), y_peer)
 
-    partner = me + 1 - 2 * (me % 2)
+    partner = partner_of(me)
     meet_neighbours(me, x_peer, y_peer, below, above, partner)
     swap = remote(other_grad, back, swap_s, swap_r, partner)
     swap.start()
@@ -856,8 +866,6 @@
         n_ref = n_pairs * (n_neg + 1)
         me = lax.axis_index('ep')
         ids = jnp.arange(group, dtype=jnp.int32)
-        partner = [(d, d + 1 - 2 * (d % 2)) for d in range(group)]
-        other_out = lax.ppermute(table_out, 'ep', partner)
 
         all_centers = trade(jnp.broadcast_to(centers[None], (group, n_pairs))).reshape(-1)
         all_owner = all_centers % group
@@ -901,7 +909,7 @@
         row4s = jnp.concatenate([refs % (2 * rows_dev) * SUB, pad])
         slot4s = jnp.concatenate([refs // (2 * rows_dev) % SLOTS * SUB, pad])
 
-        u_all, tables = gather_slots(u_mine, table_out.T, other_out.T)
+        u_all, tables = gather_slots(u_mine, table_out.T)
         own_grad, other_grad, gu, loss = score_rows(bounds, row4s, slot4s, tables, u_all)
         gu_mine, new_out = scatter_slots(gu, tables, own_grad, other_grad, width)
         new_in = add_rows(rows4, table_in, gu_mine)

time: 889 us -> 881 us (level)
  starting transfers between devices: 34.5 us -> 20.1 us
    pallas_call x1, Pallas kernels: 284 us -> 299 us  [gather_slots(): pl.pallas_call(gather_kernel, out_shape=(jax.ShapeDtypeStruct((4, 2, 2, r...]
    all_to_all x3, starting transfers between devices: 33.9 us -> 20.1 us  [trade(): return lax.all_to_all(a, 'ep', 0, 0)]
  transfers between devices with their start and end apart: 4 -> 3, of which waited for: 0 -> 0; matrix products, arithmetic and copies ran while one was open for 6% -> 1% of each run, Pallas kernels for 36% -> 70%
where the time goes in v6:
time: 881 us; the launch traced here: 871 us
  Pallas kernels  755 us (86%)
  other arithmetic  43.6 us (5%)
  local copies, waits for them, and re-layouts  34.1 us (4%)
  starting transfers between devices  20.1 us (2%)
  between operations  16.9 us (2%)
    pallas_call x1, Pallas kernels, gather_slots(): pl.pallas_call(gather_kernel, out_shape=(jax.ShapeDtypeStruct((4, 2, 2, r...  299 us
    pallas_call x1, Pallas kernels, scatter_slots(): pl.pallas_call(scatter_kernel, out_shape=(jax.ShapeDtypeStruct((rows, LAN...  285 us
    pallas_call x1, Pallas kernels, score_rows(): pl.pallas_call(score_kernel, out_shape=(half, half, jax.ShapeDtypeStruct(...  143 us
    unnamed x6, local copies, waits for them, and re-layouts  27.3 us
    all_to_all x3, starting transfers between devices, trade(): return lax.all_to_all(a, 'ep', 0, 0)  20.1 us
    sort x1, other arithmetic, device_step(): _, vals = lax.sort((keys, vals), num_keys=1, is_stable=False)  19.1 us
    pallas_call x1, Pallas kernels, add_rows(): pl.pallas_call(add_kernel, out_shape=jax.ShapeDtypeStruct(table.shape, jn...  18.7 us
  transfers between devices with their start and end apart: 3, of which 0 were waited for; matrix products, arithmetic and copies ran while one was open for 1% of the time, Pallas kernels for 70%

profile of v6, /device:TPU:0, one launch (start us, length us, event | category | flops | bytes accessed | tf_op | source)
XLA Modules:
  0.0 870.9 jit_solution(13866621606143298695)
XLA Ops:
  7.2 1.4 broadcast_in_dim.176
  8.6 7.4 all-to-all-start
  15.9 0.7 fusion.40
  16.6 0.9 pad_add_fusion.2
  18.3 9.1 %copy.111.table = f32[4096,500]{1,0:T(8,128)} copy(f32[4096,500]{0,1:T(8,128)} %param.7) | data formatting | bytes 16384000 | tf_op args[0]
  32.6 7.3 sort.29
  40.7 19.1 %sort.30 = (s32[40960]{0:T(1024)}, s32[40960]{0:T(1024)S(1)}) sort(s32[40960]{0:T(1024)S(1)} %pad_add_fusion.1, s32[40960]{0:T(1024)S(1)} %concatenate.39), dimensions={0}, to_apply=%region_6.7 | sort | flops 655360 | bytes 655360 | tf_op jit(solution)/shard_map/sort | solution.py:903
  59.8 0.6 slice.60
  60.5 5.8 all-to-all-start.1
  66.9 9.8 %pick_rows.1.mine = f32[4992,128]{1,0:T(8,128)} custom-call(s32[1248]{0:T(1024)} %fusion.38.rows4, f32[4096,500]{1,0:T(8,128)} %copy.111.table), custom_call_target="tpu_custom_call" | custom-call | tf_op jit(solution)/shard_map/pick_rows/pallas_call | solution.py:100
  76.7 298.6 %gather_slots.1 = (f32[4,2,2,4992,128]{4,3,2,1,0:T(8,128)}, f32[32768,128]{1,0:T(8,128)}, f32[500,4096]{1,0:T(8,128)}) custom-call(f32[4992,128]{1,0:T(8,128)} %pick_rows.1.mine, f32[500,4096]{1,0:T(8,128)} %bitcast.63), custom_call_target="tpu_custom_call" | custom-call | tf_op jit(solution)/shard_map/gather_slots/pallas_call | solution.py:518
  375.3 8.6 sort.31
  384.1 1.2 convert_reduce_fusion.1.bounds
  385.3 0.6 concatenate.41.slot4s
  385.9 0.6 concatenate.40.row4s
  386.6 142.7 %score_rows.1 = (f32[16384,128]{1,0:T(8,128)}, f32[16384,128]{1,0:T(8,128)}, f32[79872,128]{1,0:T(8,128)}, f32[8,128]{1,0:T(8,128)}) custom-call(s32[33]{0:T(128)} %convert_reduce_fusion.1.bounds, s32[24640]{0:T(1024)} %concatenate.40.row4s, s32[24640]{0:T(1024)} %concatenate.41.slot4s, f32[32768,128]{1,0:T(8,128)} %get-tuple-element.522.tables, ...), custom_call_target="tpu_custom_call" | custom-call | tf_op jit(solution)/shard_map/score_rows/pallas_call | solution.py:225
  529.3 1.3 slice_reduce_fusion
  531.9 6.9 all-to-all-start.2
  538.8 285.1 %scatter_slots.1 = (f32[4992,128]{1,0:T(8,128)}, f32[4096,500]{1,0:T(8,128)}, f32[16384,128]{1,0:T(8,128)}) custom-call(f32[4,2,2,4992,128]{4,3,2,1,0:T(8,128)} %bitcast.61, f32[32768,128]{1,0:T(8,128)} %get-tuple-element.522.tables, f32[16384,128]{1,0:T(8,128)} %get-tuple-element.190.own_grad, f32[16384,128]{1,0:T(8,128)} %get-tuple-element.191.other_grad), custom_call_target="tpu_custom_call" | custom-call | tf_op jit(solution)/shard_map/scatter_slots/pallas_call | solution.py:836
  823.9 18.7 %add_rows.1 = f32[4096,500]{1,0:T(8,128)} custom-call(s32[1248]{0:T(1024)} %fusion.38.rows4, f32[4096,500]{1,0:T(8,128)} %copy.111.table, f32[4992,128]{1,0:T(8,128)} %get-tuple-element.192.grads), custom_call_target="tpu_custom_call" | custom-call | tf_op jit(solution)/shard_map/add_rows/pallas_call | solution.py:127
  843.1 1.8 while.18
  843.1 1.2 slice.101
  845.0 8.9 %copy.114 = f32[4096,500]{0,1:T(8,128)} copy(f32[4096,500]{1,0:T(8,128)} %get-tuple-element.376) | data formatting | bytes 16384000
  853.8 8.9 %copy.115 = f32[4096,500]{0,1:T(8,128)} copy(f32[4096,500]{1,0:T(8,128)} %get-tuple-element.377) | data formatting | bytes 16384000
  (39 shorter events, 7.9 us)
Async XLA Ops:
  8.6 18.9 %all-to-all-start = ((s32[32,1,1024]{2,1,0:T(1,128)}), s32[32,1,1024]{2,1,0:T(1,128)S(1)}, u32[]{:S(2)}, u32[]{:S(2)}) async-start(s32[32,1,1024]{2,1,0:T(1,128)} %broadcast_in_dim.176), calls=%async_computation | async-start | bytes 262144 | tf_op jit(solution)/shard_map/all_to_all | solution.py:857
  60.5 314.9 %all-to-all-start.1 = ((s32[32,1,768]{2,1,0:T(1,128)}), s32[32,1,768]{2,1,0:T(1,128)S(1)}, u32[]{:S(2)}, u32[]{:S(2)}) async-start(s32[32,1,768]{2,1,0:T(1,128)} %bitcast.2), calls=%async_computation.1 | async-start | bytes 196608 | tf_op jit(solution)/shard_map/all_to_all | solution.py:857
  531.9 310.7 %all-to-all-start.2 = ((f32[32,1,128]{2,1,0:T(1,128)}), f32[32,1,128]{2,1,0:T(1,128)S(1)}, u32[]{:S(2)}, u32[]{:S(2)}) async-start(f32[32,1,128]{2,1,0:T(1,128)} %broadcast_in_dim.189), calls=%async_computation.2 | async-start | bytes 32768 | tf_op jit(solution)/shard_map/all_to_all | solution.py:857
  842.6 0.5 copy-start.10

commit v7 on v6

--- a/solution.py
+++ b/solution.py
@@ -377,7 +377,6 @@
     def late_out(k):
         late1_x().start()
         late1_y().start()
-        swap.start()
 
     def late_on(k):
         keep.wait()
@@ -448,6 +447,8 @@
 
     def convert(k):
         source, first = (own_t, k) if k < TURNS else (other_t, k - TURNS)
+        if k == 1:
+            swap.start()
         if k == TURNS:
             swap.wait_recv()
 

time: 881 us -> 882 us (level)
  no operation moved by 1% of the time
where the time goes in v7:
time: 882 us; the launch traced here: 871 us
  Pallas kernels  753 us (85%)
  other arithmetic  43.6 us (5%)
  local copies, waits for them, and re-layouts  34.1 us (4%)
  starting transfers between devices  22.5 us (3%)
  between operations  16.9 us (2%)
    pallas_call x1, Pallas kernels, gather_slots(): pl.pallas_call(gather_kernel, out_shape=(jax.ShapeDtypeStruct((4, 2, 2, r...  299 us
    pallas_call x1, Pallas kernels, scatter_slots(): pl.pallas_call(scatter_kernel, out_shape=(jax.ShapeDtypeStruct((rows, LAN...  285 us
    pallas_call x1, Pallas kernels, score_rows(): pl.pallas_call(score_kernel, out_shape=(half, half, jax.ShapeDtypeStruct(...  141 us
    unnamed x6, local copies, waits for them, and re-layouts  27.3 us
    all_to_all x3, starting transfers between devices, trade(): return lax.all_to_all(a, 'ep', 0, 0)  22.5 us
    sort x1, other arithmetic, device_step(): _, vals = lax.sort((keys, vals), num_keys=1, is_stable=False)  19.1 us
    pallas_call x1, Pallas kernels, add_rows(): pl.pallas_call(add_kernel, out_shape=jax.ShapeDtypeStruct(table.shape, jn...  18.6 us
  transfers between devices with their start and end apart: 3, of which 0 were waited for; matrix products, arithmetic and copies ran while one was open for 1% of the time, Pallas kernels for 70%

profile of v7, /device:TPU:0, one launch (start us, length us, event | category | flops | bytes accessed | tf_op | source)
XLA Modules:
  0.0 871.2 jit_solution(1817100190296775303)
XLA Ops:
  7.2 1.4 broadcast_in_dim.176
  8.6 7.4 all-to-all-start
  15.9 0.7 fusion.40
  16.6 0.9 pad_add_fusion.2
  18.3 9.1 %copy.111.table = f32[4096,500]{1,0:T(8,128)} copy(f32[4096,500]{0,1:T(8,128)} %param.7) | data formatting | bytes 16384000 | tf_op args[0]
  32.6 7.3 sort.29
  40.7 19.1 %sort.30 = (s32[40960]{0:T(1024)}, s32[40960]{0:T(1024)S(1)}) sort(s32[40960]{0:T(1024)S(1)} %pad_add_fusion.1, s32[40960]{0:T(1024)S(1)} %concatenate.39), dimensions={0}, to_apply=%region_6.7 | sort | flops 655360 | bytes 655360 | tf_op jit(solution)/shard_map/sort | solution.py:904
  59.8 0.6 slice.60
  60.5 5.8 all-to-all-start.1
  66.9 9.8 %pick_rows.1.mine = f32[4992,128]{1,0:T(8,128)} custom-call(s32[1248]{0:T(1024)} %fusion.38.rows4, f32[4096,500]{1,0:T(8,128)} %copy.111.table), custom_call_target="tpu_custom_call" | custom-call | tf_op jit(solution)/shard_map/pick_rows/pallas_call | solution.py:100
  76.7 298.6 %gather_slots.1 = (f32[4,2,2,4992,128]{4,3,2,1,0:T(8,128)}, f32[32768,128]{1,0:T(8,128)}, f32[500,4096]{1,0:T(8,128)}) custom-call(f32[4992,128]{1,0:T(8,128)} %pick_rows.1.mine, f32[500,4096]{1,0:T(8,128)} %bitcast.63), custom_call_target="tpu_custom_call" | custom-call | tf_op jit(solution)/shard_map/gather_slots/pallas_call | solution.py:519
  375.3 8.6 sort.31
  384.1 1.2 convert_reduce_fusion.1.bounds
  385.3 0.6 concatenate.41.slot4s
  385.9 0.6 concatenate.40.row4s
  386.6 140.8 %score_rows.1 = (f32[16384,128]{1,0:T(8,128)}, f32[16384,128]{1,0:T(8,128)}, f32[79872,128]{1,0:T(8,128)}, f32[8,128]{1,0:T(8,128)}) custom-call(s32[33]{0:T(128)} %convert_reduce_fusion.1.bounds, s32[24640]{0:T(1024)} %concatenate.40.row4s, s32[24640]{0:T(1024)} %concatenate.41.slot4s, f32[32768,128]{1,0:T(8,128)} %get-tuple-element.522.tables, ...), custom_call_target="tpu_custom_call" | custom-call | tf_op jit(solution)/shard_map/score_rows/pallas_call | solution.py:225
  527.4 1.3 slice_reduce_fusion
  530.0 9.3 %all-to-all-start.2 = ((f32[32,1,128]{2,1,0:T(1,128)}), f32[32,1,128]{2,1,0:T(1,128)S(1)}, u32[]{:S(2)}, u32[]{:S(2)}) async-start(f32[32,1,128]{2,1,0:T(1,128)} %broadcast_in_dim.189), calls=%async_computation.2 | async-start | bytes 32768 | tf_op jit(solution)/shard_map/all_to_all | solution.py:858
  539.3 285.1 %scatter_slots.1 = (f32[4992,128]{1,0:T(8,128)}, f32[4096,500]{1,0:T(8,128)}, f32[16384,128]{1,0:T(8,128)}) custom-call(f32[4,2,2,4992,128]{4,3,2,1,0:T(8,128)} %bitcast.61, f32[32768,128]{1,0:T(8,128)} %get-tuple-element.522.tables, f32[16384,128]{1,0:T(8,128)} %get-tuple-element.190.own_grad, f32[16384,128]{1,0:T(8,128)} %get-tuple-element.191.other_grad), custom_call_target="tpu_custom_call" | custom-call | tf_op jit(solution)/shard_map/scatter_slots/pallas_call | solution.py:837
  824.3 18.6 %add_rows.1 = f32[4096,500]{1,0:T(8,128)} custom-call(s32[1248]{0:T(1024)} %fusion.38.rows4, f32[4096,500]{1,0:T(8,128)} %copy.111.table, f32[4992,128]{1,0:T(8,128)} %get-tuple-element.192.grads), custom_call_target="tpu_custom_call" | custom-call | tf_op jit(solution)/shard_map/add_rows/pallas_call | solution.py:127
  843.5 1.8 while.18
  843.5 1.2 slice.101
  845.3 8.9 %copy.114 = f32[4096,500]{0,1:T(8,128)} copy(f32[4096,500]{1,0:T(8,128)} %get-tuple-element.376) | data formatting | bytes 16384000
  854.2 8.9 %copy.115 = f32[4096,500]{0,1:T(8,128)} copy(f32[4096,500]{1,0:T(8,128)} %get-tuple-element.377) | data formatting | bytes 16384000
  (39 shorter events, 7.9 us)
Async XLA Ops:
  8.6 18.9 %all-to-all-start = ((s32[32,1,1024]{2,1,0:T(1,128)}), s32[32,1,1024]{2,1,0:T(1,128)S(1)}, u32[]{:S(2)}, u32[]{:S(2)}) async-start(s32[32,1,1024]{2,1,0:T(1,128)} %broadcast_in_dim.176), calls=%async_computation | async-start | bytes 262144 | tf_op jit(solution)/shard_map/all_to_all | solution.py:858
  60.5 314.9 %all-to-all-start.1 = ((s32[32,1,768]{2,1,0:T(1,128)}), s32[32,1,768]{2,1,0:T(1,128)S(1)}, u32[]{:S(2)}, u32[]{:S(2)}) async-start(s32[32,1,768]{2,1,0:T(1,128)} %bitcast.2), calls=%async_computation.1 | async-start | bytes 196608 | tf_op jit(solution)/shard_map/all_to_all | solution.py:858
  530.0 313.0 %all-to-all-start.2 = ((f32[32,1,128]{2,1,0:T(1,128)}), f32[32,1,128]{2,1,0:T(1,128)S(1)}, u32[]{:S(2)}, u32[]{:S(2)}) async-start(f32[32,1,128]{2,1,0:T(1,128)} %broadcast_in_dim.189), calls=%async_computation.2 | async-start | bytes 32768 | tf_op jit(solution)/shard_map/all_to_all | solution.py:858
  843.0 0.5 copy-start.10
